TPU v7x, 128 devices: a whole 4x4x4 slice. The times are simulated.
128 devices in a mesh: row: 32 (over z, x, core), col: 4 (over y).
Axes of the slice: x: 4, y: 4, z: 4, core: 2. Of those that a mesh axis runs over, the one named last changes fastest.
Arguments:
- prior_scores: float32 [12288, 12288], P('row', 'col'), may hold values from 0.001 to 10
- tiles_first: bfloat16 [96, 5, 128, 128], P('row'), may hold values from 0 to 1, as said below
- columns_first: int32 [96, 5], P('row'), may hold values from 0 to 95, as said below
- tiles_second: bfloat16 [96, 5, 128, 128], P('col'), may hold values from 0 to 1, as said below
- columns_second: int32 [96, 5], P('col'), may hold values from 0 to 95, as said below
Outputs:
- alignment: float32 [12288, 12288], P('row', 'col')
Inputs may be any that keep to these rules, and one draw needn't show every extreme that they name: `tiles_first`: in every block row, the block in the first slot has entries of 0.5 or more on its diagonal. `tiles_second`: in every block row, the block in the first slot has entries of 0.5 or more on its diagonal. `columns_first`: each block row lists 5 different block columns. `columns_second`: each block row lists 5 different block columns.
All inputs are finite; a program needn't handle non-finite values.
Results may differ from a plain program's by a relative error of at most 0.0004.
The roundings to bfloat16 on the way count: a program that leaves them out, or rounds other values in their place, can miss the bound.
Values may be sent and summed in bfloat16 or wider, within the bound.
A program may use at most 192 MiB of HBM per device.

v0:
```python
import functools

import jax
import jax.numpy as jnp
from jax import lax
from jax.sharding import Mesh
from jax.sharding import PartitionSpec as P

ITERS = 2
ROW = ("row_0", "row_1", "row_2")
ROW_COL = ("row_0", "row_1", "row_2", "col")


mixing = 0.8


def by_axis(value, axes):
    return functools.reduce(lax.psum, axes, value)


def second_product(features, tile_set, columns, inverse):
    tile_size = tile_set.shape[2]
    blocks = features.reshape(-1, tile_size, features.shape[1])
    picked = jnp.take(blocks, columns, axis=0)
    result = jnp.einsum("jsoi,jsin->jon", tile_set, picked, preferred_element_type=jnp.float32)
    result = result.reshape(-1, features.shape[1]) * inverse[:, None]
    return result.astype(jnp.bfloat16)


def first_product(slab_data, tile_set, columns, inverse):
    tile_size = tile_set.shape[2]
    blocks = slab_data.reshape(slab_data.shape[0], -1, tile_size)
    picked = jnp.take(blocks, columns, axis=1)
    result = jnp.einsum("cisk,isok->cio", picked, tile_set, preferred_element_type=jnp.float32)
    result = result.reshape(slab_data.shape[0], -1) * inverse[None, :]
    return result.astype(jnp.bfloat16)


def local(prior_scores, tiles_first, columns_first, tiles_second, columns_second):
    prior_cols = prior_scores.T
    row_count = lax.axis_size(ROW)
    cell_count = float(
        prior_scores.shape[0] * row_count * prior_scores.shape[1] * lax.axis_size("col")
    )
    all_first, all_columns = (
        lax.all_gather(tiles_first, ROW, axis=0, tiled=True),
        lax.all_gather(columns_first, ROW, axis=0, tiled=True),
    )
    inverse_first = 1.0 / jnp.sum(all_first, axis=(1, 3), dtype=jnp.float32).reshape(-1)
    inverse_second = 1.0 / jnp.sum(tiles_second, axis=(1, 3), dtype=jnp.float32).reshape(-1)
    prior_sum = by_axis(jnp.sum(prior_cols), ROW_COL)
    current_state = prior_cols
    for iteration in range(ITERS):
        current = current_state.astype(jnp.bfloat16)
        gathered = lax.all_gather(current, "col", axis=0, tiled=True)
        mixed_cols = second_product(gathered, tiles_second, columns_second, inverse_second)
        slab_data = lax.all_to_all(mixed_cols, ROW, split_axis=0, concat_axis=1, tiled=True)
        propagated = first_product(slab_data, all_first, all_columns, inverse_first)
        partial_value = jnp.sum(propagated.astype(jnp.float32))
        returned = lax.all_to_all(propagated, ROW, split_axis=1, concat_axis=0, tiled=True)
        slab_sum = by_axis(partial_value, ROW_COL)
        grand_total = mixing * slab_sum + (1.0 - mixing) * prior_sum
        updated = mixing * returned.astype(jnp.float32) + (1.0 - mixing) * prior_cols
        current_state = updated / (grand_total / cell_count)
    return current_state.T


def solution(mesh):
    finer = Mesh(
        mesh.devices.reshape(4, 4, 2, mesh.shape["col"]), ("row_0", "row_1", "row_2", "col")
    )
    return jax.shard_map(
        local,
        mesh=finer,
        in_specs=(
            P(ROW, "col"),
            P(ROW, None, None, None),
            P(ROW, None),
            P("col", None, None, None),
            P("col", None),
        ),
        out_specs=P(ROW, "col"),
        check_vma=False,
    )
```

profile of v0, /device:TPU:1, one launch (start us, length us, event | category | flops | bytes accessed | tf_op | source)
XLA Modules:
  0.0 632.9 jit_solution(3991835615490677281)
XLA Ops:
  17.4 91.3 %all-gather.5.cloned.1.call-done = bf16[12288,384]{0,1:T(8,128)(2,1)} async-done(((bf16[3072,384]{0,1:T(8,128)(2,1)}), bf16[12288,384]{0,1:T(8,128)(2,1)}) %all-gather.5.cloned.1.call-update) | async-done | bytes 9437200 | tf_op jit(solution)/shard_map/all_gather | solution.py:55
  108.7 12.6 %copy.59 = bf16[12288,384]{1,0:T(8,128)(2,1)} copy(bf16[12288,384]{0,1:T(8,128)(2,1)} %all-gather.5.cloned.1.call-done) | data formatting | bytes 18874368 | tf_op jit(solution)/shard_map/all_gather | solution.py:55
  121.3 12.8 %gather_fusion = bf16[120,128,384]{2,1,0:T(8,128)(2,1)} fusion(bf16[96,128,384]{2,1,0:T(8,128)(2,1)} %bitcast.69, s32[1024]{0:T(1024)S(1)} %pad_clamp_fusion.1), kind=kCustom, calls=%fused_computation.clone | custom fusion | bytes 23593440 | tf_op jit(solution)/shard_map/jit(_take)/gather | solution.py:24
  134.1 8.2 %fusion.8 = f32[24,384,128,1]{1,2,3,0:T(8,128)S(1)} fusion(bf16[24,5,128,128]{3,2,1,0:T(8,128)(2,1)} %param.12, bf16[24,5,128,384]{3,2,1,0:T(8,128)(2,1)} %bitcast.75, pred[24,5]{1,0:T(8,128)(4,1)S(1)} %copy.56), kind=kOutput, calls=%fused_computation.13 | convolution fusion | flops 1515847680 | bytes 20447352 | tf_op jit(solution)/shard_map/jsoi,jsin->jon/dot_general | solution.py:25
  144.2 7.8 %all-to-all-start = ((bf16[32,96,384]{2,1,0:T(8,128)(2,1)}), bf16[32,96,384]{2,1,0:T(8,128)(2,1)S(1)}, u32[]{:S(2)}, u32[]{:S(2)}) async-start(bf16[32,96,384]{2,1,0:T(8,128)(2,1)} %multiply_convert_fusion.5), calls=%async_computation | async-start | bytes 4718592 | tf_op jit(solution)/shard_map/all_to_all | solution.py:57
  152.0 70.7 %all-gather = s32[32,3,5]{2,1,0:T(4,128)S(1)} all-gather(s32[1,3,5]{2,1,0:T(4,128)S(1)} %bitcast.80), channel_id=1, replica_groups=mesh['row_0'=4,'row_1'=4,'row_2'=2,'col'=4] {'row_0','row_1','row_2'}, dimensions={0}, use_global_device_ids=true | all-gather | bytes 1980 | tf_op jit(solution)/shard_map/all_gather | solution.py:47
  233.5 14.9 %gather_fusion.1 = bf16[480,96,128]{2,1,0:T(8,128)(2,1)} fusion(bf16[96,96,128]{2,0,1:T(8,128)(2,1)S(1)} %copy.63, s32[1024]{0:T(1024)S(1)} %pad_clamp_fusion), kind=kCustom, calls=%fused_computation.1.clone | custom fusion | bytes 23594880 | tf_op jit(solution)/shard_map/jit(_take)/gather | solution.py:33
  255.0 14.1 %convert_reduce_fusion.3 = (f32[]{:T(128)}, f32[96,96,128]{2,0,1:T(8,128)}) fusion(f32[96,128]{1,0:T(8,128)S(1)} %broadcast_divide_fusion, bf16[96,5,128,128]{3,2,1,0:T(8,128)(2,1)} %all-gather.7.cloned.1.call-done, bf16[96,5,96,128]{3,2,1,0:T(8,128)(2,1)} %bitcast.70, pred[96,5]{1,0:T(8,128)(4,1)S(1)} %copy.55), kind=kOutput, calls=%fused_computation.34 | convolution fusion | flops 1520566272 | bytes 32293348 | tf_op jit(solution)/shard_map/cisk,isok->cio/dot_general | solution.py:34
  269.1 7.2 %copy.64 = f32[96,96,128]{2,1,0:T(8,128)} copy(f32[96,96,128]{2,0,1:T(8,128)} %get-tuple-element.18) | data formatting | bytes 9437184 | tf_op jit(solution)/shard_map/cisk,isok->cio/transpose | solution.py:34
  298.9 22.7 %all-reduce.2 = (f32[]{:T(128)}, f32[]{:T(128)}) all-reduce(f32[]{:T(128)} %get-tuple-element.17, f32[]{:T(128)} %get-tuple-element.15), channel_id=1, replica_groups=mesh['row_0'=4,'row_1'=4,'row_2'=2,'col'=4] {'row_0'}, use_global_device_ids=true, to_apply=%region_3.6 | all-reduce | flops 2 | bytes 16 | tf_op jit(solution)/shard_map/psum | solution.py:18
  321.5 9.5 %all-reduce.1 = (f32[]{:T(128)}, f32[]{:T(128)}) all-reduce(f32[]{:T(128)} %get-tuple-element.11, f32[]{:T(128)} %get-tuple-element.12), channel_id=1, replica_groups=mesh['row_0'=4,'row_1'=4,'row_2'=2,'col'=4] {'row_1'}, use_global_device_ids=true, to_apply=%region_4.7 | all-reduce | flops 2 | bytes 16 | tf_op jit(solution)/shard_map/psum | solution.py:18
  331.0 7.6 %all-reduce.3 = (f32[]{:T(128)}, f32[]{:T(128)}) all-reduce(f32[]{:T(128)} %get-tuple-element.9, f32[]{:T(128)} %get-tuple-element.10), channel_id=1, replica_groups=mesh['row_0'=4,'row_1'=4,'row_2'=2,'col'=4] {'row_2'}, use_global_device_ids=true, to_apply=%region_5.8 | all-reduce | flops 2 | bytes 16 | tf_op jit(solution)/shard_map/psum | solution.py:18
  338.7 9.1 %all-reduce = (f32[]{:T(128)}, f32[]{:T(128)}) all-reduce(f32[]{:T(128)} %get-tuple-element.13, f32[]{:T(128)} %get-tuple-element.14), channel_id=1, replica_groups=mesh['row_0'=4,'row_1'=4,'row_2'=2,'col'=4] {'col'}, use_global_device_ids=true, to_apply=%region_6.9 | all-reduce | flops 2 | bytes 16 | tf_op jit(solution)/shard_map/psum | solution.py:18
  353.5 88.1 %all-gather.9.cloned.1.call-done = bf16[12288,384]{1,0:T(8,128)(2,1)} async-done(((bf16[3072,384]{1,0:T(8,128)(2,1)}), bf16[12288,384]{1,0:T(8,128)(2,1)}) %all-gather.9.cloned.1.call-update) | async-done | bytes 9437200 | tf_op jit(solution)/shard_map/all_gather | solution.py:55
  441.6 12.3 %gather_fusion.2 = bf16[120,128,384]{2,1,0:T(8,128)(2,1)} fusion(bf16[96,128,384]{2,1,0:T(8,128)(2,1)} %bitcast.73, s32[1024]{0:T(1024)S(1)} %pad_clamp_fusion.1), kind=kCustom, calls=%fused_computation.2.clone | custom fusion | bytes 23593440 | tf_op jit(solution)/shard_map/jit(_take)/gather | solution.py:24
  453.9 8.2 %fusion.5 = f32[24,384,128,1]{1,2,3,0:T(8,128)S(1)} fusion(bf16[24,5,128,128]{3,2,1,0:T(8,128)(2,1)} %param.12, bf16[24,5,128,384]{3,2,1,0:T(8,128)(2,1)} %bitcast.74, pred[24,5]{1,0:T(8,128)(4,1)S(1)} %copy.56), kind=kOutput, calls=%fused_computation.10 | convolution fusion | flops 1515847680 | bytes 20447352 | tf_op jit(solution)/shard_map/jsoi,jsin->jon/dot_general | solution.py:25
  462.6 39.2 %all_to_all.46 = bf16[32,96,384]{2,1,0:T(8,128)(2,1)S(1)} all-to-all(bf16[32,96,384]{2,1,0:T(8,128)(2,1)S(1)} %multiply_convert_fusion.2), channel_id=1, replica_groups=mesh['row_0'=4,'row_1'=4,'row_2'=2,'col'=4] {'row_0','row_1','row_2'}, dimensions={0} | all-to-all | bytes 4718592 | tf_op jit(solution)/shard_map/all_to_all | solution.py:57
  507.8 14.9 %gather_fusion.3 = bf16[480,96,128]{2,1,0:T(8,128)(2,1)} fusion(bf16[96,96,128]{2,0,1:T(8,128)(2,1)S(1)} %copy.70, s32[1024]{0:T(1024)S(1)} %pad_clamp_fusion), kind=kCustom, calls=%fused_computation.3.clone | custom fusion | bytes 23594880 | tf_op jit(solution)/shard_map/jit(_take)/gather | solution.py:33
  522.6 14.2 %convert_reduce_fusion.2 = (f32[]{:T(128)}, f32[96,96,128]{2,0,1:T(8,128)}) fusion(f32[96,128]{1,0:T(8,128)S(1)} %broadcast_divide_fusion, bf16[96,5,128,128]{3,2,1,0:T(8,128)(2,1)} %all-gather.7.cloned.1.call-done, bf16[96,5,96,128]{3,2,1,0:T(8,128)(2,1)} %bitcast.71, pred[96,5]{1,0:T(8,128)(4,1)S(1)} %copy.55), kind=kOutput, calls=%fused_computation.29 | convolution fusion | flops 1520566272 | bytes 32293348 | tf_op jit(solution)/shard_map/cisk,isok->cio/dot_general | solution.py:34
  536.9 7.2 %copy.71 = f32[96,96,128]{2,1,0:T(8,128)} copy(f32[96,96,128]{2,0,1:T(8,128)} %get-tuple-element.20) | data formatting | bytes 9437184 | tf_op jit(solution)/shard_map/cisk,isok->cio/transpose | solution.py:34
  559.2 28.8 %psum.92 = f32[]{:T(128)} all-reduce(f32[]{:T(128)} %get-tuple-element.19), channel_id=1, replica_groups=mesh['row_0'=4,'row_1'=4,'row_2'=2,'col'=4] {'row_0'}, use_global_device_ids=true, to_apply=%region_13.16 | all-reduce | flops 1 | bytes 8 | tf_op jit(solution)/shard_map/psum | solution.py:18
  588.0 9.5 %psum.93 = f32[]{:T(128)} all-reduce(f32[]{:T(128)} %psum.92), channel_id=1, replica_groups=mesh['row_0'=4,'row_1'=4,'row_2'=2,'col'=4] {'row_1'}, use_global_device_ids=true, to_apply=%region_14.17 | all-reduce | flops 1 | bytes 8 | tf_op jit(solution)/shard_map/psum | solution.py:18
  597.5 7.6 %psum.94 = f32[]{:T(128)} all-reduce(f32[]{:T(128)} %psum.93), channel_id=1, replica_groups=mesh['row_0'=4,'row_1'=4,'row_2'=2,'col'=4] {'row_2'}, use_global_device_ids=true, to_apply=%region_15.18 | all-reduce | flops 1 | bytes 8 | tf_op jit(solution)/shard_map/psum | solution.py:18
  605.0 8.1 %psum.95 = f32[]{:T(128)} all-reduce(f32[]{:T(128)} %psum.94), channel_id=1, replica_groups=mesh['row_0'=4,'row_1'=4,'row_2'=2,'col'=4] {'col'}, use_global_device_ids=true, to_apply=%region_16.19 | all-reduce | flops 1 | bytes 8 | tf_op jit(solution)/shard_map/psum | solution.py:18
  (59 shorter events, 90.9 us)
Async XLA Ops:
  6.5 7.8 %copy-start.1 = (s32[24,5]{0,1:T(8,128)S(1)}, s32[24,5]{0,1:T(8,128)}, u32[]{:S(2)}) copy-start(s32[24,5]{0,1:T(8,128)} %param.13) | copy-start | bytes 1444
  6.5 102.1 %all-gather.5.cloned.1.call-start = ((), (), s32[]{:S(2)}) async-start(), calls=%async_computation.4 | async-start | bytes 11796480 | tf_op jit(solution)/shard_map/all_gather | solution.py:55
  13.5 234.8 %all-gather.7.cloned.1.call-start = ((), (), s32[]{:S(2)}) async-start(), calls=%async_computation.5 | async-start | bytes 16220160 | tf_op jit(solution)/shard_map/all_gather | solution.py:46
  142.3 9.7 %copy-start.2 = (s32[3,5]{1,0:T(4,128)S(1)}, s32[3,5]{1,0:T(4,128)}, u32[]{:S(2)}) copy-start(s32[3,5]{1,0:T(4,128)} %param.11) | copy-start | bytes 184
  144.2 79.0 %all-to-all-start = ((bf16[32,96,384]{2,1,0:T(8,128)(2,1)}), bf16[32,96,384]{2,1,0:T(8,128)(2,1)S(1)}, u32[]{:S(2)}, u32[]{:S(2)}) async-start(bf16[32,96,384]{2,1,0:T(8,128)(2,1)} %multiply_convert_fusion.5), calls=%async_computation | async-start | bytes 4718592 | tf_op jit(solution)/shard_map/all_to_all | solution.py:57
  287.6 61.4 %all-to-all-start.1 = ((bf16[96,32,384]{2,0,1:T(8,128)(2,1)}), bf16[96,32,384]{2,0,1:T(8,128)(2,1)S(1)}, u32[]{:S(2)}, u32[]{:S(2)}) async-start(bf16[96,32,384]{2,0,1:T(8,128)(2,1)} %copy.65), calls=%async_computation.1 | async-start | bytes 4718592 | tf_op jit(solution)/shard_map/all_to_all | solution.py:60
  292.8 148.8 %all-gather.9.cloned.1.call-start = ((), (), s32[]{:S(2)}) async-start(), calls=%async_computation.6 | async-start | bytes 11796480 | tf_op jit(solution)/shard_map/all_gather | solution.py:55
  349.1 2.3 copy-start
  555.3 58.4 %all-to-all-start.3 = ((bf16[96,32,384]{2,0,1:T(8,128)(2,1)}), bf16[96,32,384]{2,0,1:T(8,128)(2,1)S(1)}, u32[]{:S(2)}, u32[]{:S(2)}) async-start(bf16[96,32,384]{2,0,1:T(8,128)(2,1)} %copy.72), calls=%async_computation.3 | async-start | bytes 4718592 | tf_op jit(solution)/shard_map/all_to_all | solution.py:60
Sparse Core Ops, SparseCore 0:
  13.7 94.9 all-gather.4
  110.9 96.5 all-gather.6
  353.6 87.9 all-gather.8
where the time goes:
time: 642 us; the launch traced here: 633 us
  blocking collectives  213 us (33%)
  waiting for transfers between devices  180 us (28%)
  local copies, waits for them, and re-layouts  129 us (20%)
  matrix products  44.8 us (7%)
  other arithmetic  33.4 us (5%)
  starting transfers between devices  16.9 us (3%)
  between operations  15.6 us (2%)
    all_gather x2, waiting for transfers between devices, local(): gathered = lax.all_gather(current, 'col', axis=0, tiled=True)  179 us
    psum x8, blocking collectives, by_axis(): return functools.reduce(lax.psum, axes, value)  103 us
    all_gather x1, blocking collectives, local(): lax.all_gather(columns_first, ROW, axis=0, tiled=True)  70.7 us
    all_to_all x1, blocking collectives, local(): lax.all_to_all(mixed_cols, ROW, split_axis=0, concat_axis=1, tiled=True)  39.2 us
    gather x2, local copies, waits for them, and re-layouts, first_product(): picked = jnp.take(blocks, columns, axis=1)  29.8 us
    dot_general x2, matrix products, first_product(): jnp.einsum('cisk,isok->cio', picked, tile_set, preferred_element_type=jnp...  28.3 us
    gather x2, local copies, waits for them, and re-layouts, second_product(): picked = jnp.take(blocks, columns, axis=0)  25.1 us
    dot_general x2, matrix products, second_product(): jnp.einsum('jsoi,jsin->jon', tile_set, picked, preferred_element_type=jnp...  16.5 us
  transfers between devices with their start and end apart: 6, of which 2 were waited for; matrix products, arithmetic and copies ran while one was open for 11% of the time, Pallas kernels for 0%

commit v1 on v0

v1 whole, which is shorter than its diff:
```python
import functools

import jax
import jax.numpy as jnp
from jax import lax
from jax.experimental import pallas as pl
from jax.experimental.pallas import tpu as pltpu
from jax.sharding import PartitionSpec as P

MESH = pl.DeviceIdType.MESH
BF = jnp.bfloat16
F32 = jnp.float32
MIX = 0.8
CELLS = float(12288 * 12288)
NT = (((1,), (1,)), ((), ()))
NN = (((1,), (0,)), ((), ()))


def half_lanes(shape):
    return lax.broadcasted_iota(jnp.int32, shape, 1) < 64


def swap(value):
    return pltpu.roll(value, 64, 1)


def main_kernel(
    prior, t1, t2, c1, c2,
    outf, outp, mout,
    prior_r, a1, a2, xr, zc, zpk, zsend, zspk, pfull, ppk, ph, prf, prp,
    mbuf, mpart, mtot, macc, c1g, c2g, c1s, c2s,
    lsem, ps_sem, pr_sem, cs_sem, cr_sem, ds_sem, dr_sem,
    gs_sem, gr_sem, xs_sem, xf_sem,
    zs_sem, zr_sem, fs_sem, ff_sem,
    qs_sem, qr_sem, os_sem, or_sem, ms_sem, mr_sem, mts_sem, mtr_sem,
):
    row = lax.axis_index("row")
    y = lax.axis_index("col")
    k = row % 2
    s = row // 2
    x = s % 4
    z = s // 4
    me = s * 4 + y

    def dev(s_, y_, k_):
        return {"row": s_ * 2 + k_, "col": y_}

    def remote(src, dst, ssem, rsem, target):
        return pltpu.make_async_remote_copy(
            src_ref=src, dst_ref=dst, send_sem=ssem, recv_sem=rsem,
            device_id=target, device_id_type=MESH,
        )

    barrier = pltpu.get_barrier_semaphore()

    def greet(i, _):
        other = (row * 4 + y + i) % 128
        pl.semaphore_signal(
            barrier, inc=1, device_id={"row": other // 4, "col": other % 4}, device_id_type=MESH
        )
        return 0

    load1 = pltpu.make_async_copy(t1, a1.at[pl.ds(s * 1920, 1920)], lsem.at[0])
    load1.start()
    load2 = pltpu.make_async_copy(t2.at[pl.ds(k * 7680, 7680)], a2.at[0], lsem.at[1])
    load2.start()
    load3 = pltpu.make_async_copy(
        prior.at[:, pl.ds(pl.multiple_of(y * 32, 32), 32), :], prior_r.at[y], lsem.at[2]
    )
    load3.start()
    lax.fori_loop(1, 128, greet, 0)
    c1g[s] = c1[...]
    c2g[y] = c2[...]
    xr[:, 192:208, :] = jnp.ones((96, 16, 128), BF)
    pl.semaphore_wait(barrier, 127)

    slice_copies, prior_copies, col_copies = [], [], []
    for d in (1, 3, 2):
        yd = (y + d) % 4
        cp = remote(
            t2.at[pl.ds(k * 7680 + s * 480, 480)],
            a2.at[(4 - d) % 4, pl.ds(s * 480, 480)],
            ds_sem.at[d], dr_sem.at[d], dev(s, yd, k),
        )
        cp.start()
        slice_copies.append(cp)
        cc = remote(c2, c2g.at[y], cs_sem.at[16 + d], cr_sem.at[16 + d], dev(s, yd, k))
        cc.start()
        col_copies.append(cc)

    XP, XM = (z * 4 + (x + 1) % 4), (z * 4 + (x + 3) % 4)
    ZP, ZM = (((z + 1) % 4) * 4 + x), (((z + 3) % 4) * 4 + x)

    def region(kind, origin, part):
        if kind == 0:
            off, size = ((0, 480), (480, 480), (960, 480), (1440, 480), (0, 960), (960, 960))[part]
            return a1.at[pl.ds(pl.multiple_of(origin * 1920 + off, 16), size)]
        off, size = ((0, 128), (128, 112), (240, 128), (368, 112), (0, 240), (240, 240))[part]
        return a2.at[pl.ds(1, 3), pl.ds(pl.multiple_of(origin * 480 + off, 16), size)]

    def nbr(axis, up):
        return (XP if up else XM) if axis == 0 else (ZP if up else ZM)

    def shifted(axis, origin, delta):
        ox, oz = origin % 4, origin // 4
        if axis == 0:
            return oz * 4 + (ox + delta) % 4
        return ((oz + delta) % 4) * 4 + ox

    gather_copies = []

    def hop(kind, half, group, slot, origin, part, axis, up):
        cp = remote(
            region(kind, origin, part), region(kind, origin, part),
            gs_sem.at[kind, half, group, slot], gr_sem.at[kind, half, group, slot],
            dev(nbr(axis, up), y, k),
        )
        cp.start()
        gather_copies.append(cp)

    def landed(kind, half, group, slot, origin, part):
        cp = remote(
            region(kind, origin, part), region(kind, origin, part),
            gs_sem.at[kind, half, group, slot], gr_sem.at[kind, half, group, slot],
            dev(nbr(0, True), y, k),
        )
        cp.wait_recv()

    def whole(half):
        return 4 + half

    def ring_start(kind, half, group, origin, axis):
        hop(kind, half, group, 0, origin, whole(half), axis, True)
        hop(kind, half, group, 1, origin, whole(half), axis, False)

    def ring_relay(kind, half, group, base, axis):
        low, high = shifted(axis, base, 3), shifted(axis, base, 1)
        landed(kind, half, group, 0, low, whole(half))
        hop(kind, half, group, 2, low, 2 * half, axis, True)
        landed(kind, half, group, 1, high, whole(half))
        hop(kind, half, group, 3, high, 2 * half + 1, axis, False)

    def ring_end(kind, half, group, base, axis):
        far = shifted(axis, base, 2)
        landed(kind, half, group, 2, far, 2 * half)
        landed(kind, half, group, 3, far, 2 * half + 1)

    def stage1(kind):
        for half in (0, 1):
            ring_start(kind, half, 0, s, half)
        for half in (0, 1):
            ring_start(kind, half, 1, s, 1 - half)

    def stage2(kind):
        for half in (0, 1):
            ring_relay(kind, half, 0, s, half)
            for g, delta in ((2, 3), (3, 1)):
                ring_start(kind, half, g, shifted(half, s, delta), 1 - half)

    def stage3(kind):
        for half in (0, 1):
            ring_end(kind, half, 0, s, half)
            ring_start(kind, half, 4, shifted(half, s, 2), 1 - half)

    def stage4(kind):
        for g, delta in ((1, 0), (2, 3), (3, 1), (4, 2)):
            for half in (0, 1):
                ring_relay(kind, half, g, shifted(half, s, delta), 1 - half)

    def stage5(kind):
        for g, delta in ((1, 0), (2, 3), (3, 1), (4, 2)):
            for half in (0, 1):
                ring_end(kind, half, g, shifted(half, s, delta), 1 - half)

    load1.wait()
    stage1(0)
    for d in (1, 3, 2):
        yd = (y + d) % 4
        cp = remote(
            prior.at[:, pl.ds(pl.multiple_of(yd * 32, 32), 32), :], prior_r.at[y],
            ps_sem.at[d], pr_sem.at[d], dev(s, yd, k),
        )
        cp.start()
        prior_copies.append(cp)

    def send_columns(i, _):
        remote(
            c1, c1g.at[s], cs_sem.at[i], cr_sem.at[i], dev((s + i) % 16, y, k)
        ).start()
        return 0

    lax.fori_loop(1, 16, send_columns, 0)

    for cp in slice_copies:
        cp.wait()
    stage1(1)
    stage2(0)
    stage2(1)
    stage3(0)
    stage3(1)
    load3.wait()
    load2.wait()

    for cc in col_copies:
        cc.wait()

    def wait_columns(i, _):
        remote(
            c1, c1g.at[(s + 16 - i) % 16], cs_sem.at[i], cr_sem.at[i], dev((s + i) % 16, y, k)
        ).wait()
        return 0

    lax.fori_loop(1, 16, wait_columns, 0)
    cps = [
        pltpu.make_async_copy(c1g, c1s, lsem.at[3]),
        pltpu.make_async_copy(c2g, c2s, lsem.at[4]),
    ]
    for cp in cps:
        cp.start()
    for cp in cps:
        cp.wait()

    stage4(1)
    stage4(0)
    for cp in prior_copies:
        cp.wait()

    mask96 = half_lanes((96, 128))
    mask48 = half_lanes((48, 128))

    def forward_state(group):
        return remote(
            xr.at[pl.ds(group * 3, 3), pl.ds(k * 96, 96)],
            xr.at[pl.ds(group * 3, 3), pl.ds(k * 96, 96)],
            xs_sem.at[group], xf_sem.at[group], dev(s, y, 1 - k),
        )

    def state_wait(group):
        remote(
            xr.at[pl.ds(group * 3, 3), pl.ds((1 - k) * 96, 96)],
            xr.at[pl.ds(group * 3, 3), pl.ds((1 - k) * 96, 96)],
            xs_sem.at[group], xf_sem.at[group], dev(s, y, 1 - k),
        ).wait()

    macc[...] = jnp.zeros((8, 128), F32)

    def convert(group, _):
        ys = group // 8
        for t in range(3):
            col = pl.multiple_of((group % 8) * 384 + t * 128, 128)
            value = prior_r[ys, :, :, pl.ds(col, 128)].reshape(96, 128)
            macc[...] += jnp.sum(value.reshape(12, 8, 128), axis=0)
            xr[group * 3 + t, pl.ds(pl.multiple_of(k * 96, 16), 96), :] = value.astype(BF)

        @pl.when(group > 0)
        def _():
            forward_state(group - 1).start()

        return 0

    lax.fori_loop(0, 32, convert, 0)
    forward_state(31).start()
    stage5(1)

    def state_done(group, _):
        state_wait(group)
        return 0

    def z_places(src_s, src_y, p):
        return (
            (
                pl.ds((src_s * 2 + p) * 3, 3),
                pl.ds(pl.multiple_of(src_y * 32, 32), 32),
                pl.ds(0, 128),
            ),
            (
                pl.ds(src_s * 3, 3),
                pl.ds(pl.multiple_of(src_y * 32 + p * 16, 16), 16),
                pl.ds(0, 128),
            ),
        )

    def z_copies(i, fn):
        yd = (y + i // 4) % 4
        g = (i + s) % 4
        for d in range(2):
            sd = k * 8 + g * 2 + d
            slot = yd * 8 + g * 2 + d
            for p in range(2):
                self_part = jnp.logical_and(jnp.logical_and(sd == s, yd == y), k == p)
                full_at, packed_at = z_places(s, y, p)
                full = remote(
                    zsend.at[slot, p], zc.at[full_at],
                    zs_sem.at[slot, p, 0], zr_sem.at[me, 0], dev(sd, yd, p),
                )
                packed = remote(
                    zspk.at[slot, :, pl.ds(p * 16, 16), :], zpk.at[packed_at],
                    zs_sem.at[slot, p, 1], zr_sem.at[me, 1], dev(sd, yd, p),
                )

                @pl.when(jnp.logical_not(self_part))
                def _():
                    fn(full)
                    fn(packed)

                if fn is begin:

                    @pl.when(self_part)
                    def _():
                        zc[full_at] = zsend[slot, p]
                        zpk[packed_at] = zspk[slot, :, p * 16 : p * 16 + 16, :]

    def begin(cp):
        cp.start()

    def end_send(cp):
        cp.wait_send()

    def z_compute(i, _):
        yd = (y + i // 4) % 4
        g = (i + s) % 4
        yr = i // 4
        values = []
        for t in range(3):
            jl = g * 3 + t
            acc = None
            for slot in range(5):
                c = c2s[yd, k * 12 + jl, slot]
                tile = a2[yr, pl.ds(pl.multiple_of((jl * 5 + slot) * 128, 128), 128), :]
                part = lax.dot_general(xr[c], tile, NT, preferred_element_type=F32)
                acc = part if acc is None else acc + part
            inv = 1.0 / acc[192:193, :]
            values.append(acc[0:192, :] * inv)
        out = yd * 8 + g * 2
        for p in range(2):
            rows = slice(p * 96, p * 96 + 96)
            zsend[out, p] = values[0][rows].astype(BF).reshape(3, 32, 128)
            zsend[out + 1, p] = values[2][rows].astype(BF).reshape(3, 32, 128)
        top, bottom = values[1][0:96], values[1][96:192]
        even = jnp.where(mask96, top, swap(bottom))
        odd = jnp.where(mask96, swap(top), bottom)
        zspk[out] = even.astype(BF).reshape(3, 32, 128)
        zspk[out + 1] = odd.astype(BF).reshape(3, 32, 128)

        @pl.when(i > 0)
        def _():
            z_copies(i - 1, begin)

        return 0

    def z_forward(src_s, src_y):
        src = src_s * 4 + src_y
        full_at, packed_at = z_places(src_s, src_y, k)
        full = remote(
            zc.at[full_at], zc.at[full_at],
            fs_sem.at[src, 0], ff_sem.at[src, 0], dev(s, y, 1 - k),
        )
        packed = remote(
            zpk.at[packed_at], zpk.at[packed_at],
            fs_sem.at[src, 1], ff_sem.at[src, 1], dev(s, y, 1 - k),
        )
        return full, packed

    def z_receive(i, _):
        src_s = (s + i // 4) % 16
        src_y = (y + i) % 4
        src = src_s * 4 + src_y
        full, packed = z_forward(src_s, src_y)
        own = jnp.logical_and(src == me, s // 8 == k)

        @pl.when(jnp.logical_not(own))
        def _():
            full_at, packed_at = z_places(src_s, src_y, k)
            remote(
                zc.at[full_at], zc.at[full_at],
                fs_sem.at[src, 0], zr_sem.at[src, 0], dev(s, y, 1 - k),
            ).wait_recv()
            remote(
                zpk.at[packed_at], zpk.at[packed_at],
                fs_sem.at[src, 1], zr_sem.at[src, 1], dev(s, y, 1 - k),
            ).wait_recv()

        full.start()
        packed.start()
        return 0

    def z_finish(i, _):
        src_s = (s + i // 4) % 16
        src_y = (y + i) % 4
        src = src_s * 4 + src_y
        full_at, packed_at = z_places(src_s, src_y, 1 - k)
        remote(
            zc.at[full_at], zc.at[full_at],
            fs_sem.at[src, 0], ff_sem.at[src, 0], dev(s, y, 1 - k),
        ).wait()
        remote(
            zpk.at[packed_at], zpk.at[packed_at],
            fs_sem.at[src, 1], ff_sem.at[src, 1], dev(s, y, 1 - k),
        ).wait()
        return 0

    def z_unpack(i, _):
        packed = zpk[i].astype(F32)
        lane = lax.broadcasted_iota(jnp.int32, (128, 128), 1)
        fill = jnp.where(lane == 64, 1.0, 0.0).astype(F32)
        block = (i // 3) * 6 + i % 3
        zc[block, :, 128:256] = jnp.where(lane < 64, packed, fill).astype(BF)
        zc[block + 3, :, 128:256] = jnp.where(lane < 64, swap(packed), fill).astype(BF)
        return 0

    def second_stage():
        lax.fori_loop(0, 32, state_done, 0)
        lax.fori_loop(0, 16, z_compute, 0)
        z_copies(15, begin)
        lax.fori_loop(0, 64, z_receive, 0)
        lax.fori_loop(0, 64, z_finish, 0)

        def sent(i, _):
            z_copies(i, end_send)
            return 0

        lax.fori_loop(0, 16, sent, 0)
        lax.fori_loop(0, 48, z_unpack, 0)

    def p_copies(i, last, fn):
        sd = (s + i) % 16
        if last:
            full = (pfull.at[pl.ds(sd * 3, 3)], outf.at[s])
            packed = (ppk.at[sd], outp.at[s])
            pair = [
                remote(*full, os_sem.at[sd, 0], or_sem.at[s, 0], dev(sd, y, k)),
                remote(*packed, os_sem.at[sd, 1], or_sem.at[s, 1], dev(sd, y, k)),
            ]
            mine = [
                pltpu.make_async_copy(*full, lsem.at[5]),
                pltpu.make_async_copy(*packed, lsem.at[6]),
            ]

            @pl.when(sd != s)
            def _():
                for cp in pair:
                    fn(cp)

            @pl.when(sd == s)
            def _():
                for cp in mine:
                    if fn is begin:
                        cp.start()
                    else:
                        cp.wait()

            return
        for yd in range(4):
            own = jnp.logical_and(sd == s, y == yd)
            pair = [
                remote(
                    pfull.at[pl.ds(sd * 3, 3), pl.ds(yd * 32, 32)], prf.at[me],
                    qs_sem.at[sd * 4 + yd, 0], qr_sem.at[me, 0], dev(sd, yd, k),
                ),
                remote(
                    ppk.at[sd, yd], prp.at[me],
                    qs_sem.at[sd * 4 + yd, 1], qr_sem.at[me, 1], dev(sd, yd, k),
                ),
            ]

            @pl.when(jnp.logical_not(own))
            def _():
                for cp in pair:
                    fn(cp)

            if fn is begin:

                @pl.when(own)
                def _():
                    prf[me] = pfull[pl.ds(sd * 3, 3), pl.ds(yd * 32, 32), :]
                    prp[me] = ppk[sd, yd]

    def p_compute(last, i, _):
        sd = (s + i) % 16
        for t in range(3):
            acc = None
            for slot in range(5):
                c = c1s[sd, t, slot]
                tile = a1[pl.ds(pl.multiple_of((sd * 15 + t * 5 + slot) * 128, 128), 128), :]
                part = lax.dot_general(
                    tile, zc[c], NN, preferred_element_type=F32
                )
                acc = part if acc is None else acc + part
            inv = 1.0 / acc[:, 192:193]
            first = (acc[:, 0:128] * inv).astype(BF)
            second = (acc[:, 128:256] * inv).astype(BF).astype(F32)
            second = jnp.where(half_lanes((128, 128)), second, 0.0)
            total = first.astype(F32) + second
            mpart[...] += jnp.sum(total.reshape(16, 8, 128), axis=0)
            pfull[sd * 3 + t] = first
            ph[t] = second
        for yd in range(4):
            if last:
                flat = ph[...].reshape(384, 128)
                low = flat[yd * 48 : yd * 48 + 48]
                high = flat[192 + yd * 48 : 240 + yd * 48]
            else:
                low = ph[:, yd * 32 : yd * 32 + 16, :].reshape(48, 128)
                high = ph[:, yd * 32 + 16 : yd * 32 + 32, :].reshape(48, 128)
            ppk[sd, yd] = (low + swap(high)).astype(BF)

        @pl.when(i > 0)
        def _():
            p_copies(i - 1, last, begin)

        return 0

    def first_stage(last, it):
        mpart[...] = jnp.zeros((8, 128), F32)
        lax.fori_loop(0, 16, functools.partial(p_compute, last), 0)
        p_copies(15, last, begin)
        mbuf[it, me] = MIX * mpart[...] + (1.0 - MIX) * macc[...]
        mpart[...] = mbuf[it, me]

        def total_copy(i, src, dst):
            other = (me + i) % 64
            return remote(
                mpart, mbuf.at[it, src], ms_sem.at[i], mr_sem.at[i], dev(dst // 4, dst % 4, k)
            )

        def total_send(i, _):
            total_copy(i, me, (me + i) % 64).start()
            return 0

        def total_wait(i, _):
            total_copy(i, (me + 64 - i) % 64, (me + i) % 64).wait()
            return 0

        lax.fori_loop(1, 64, total_send, 0)
        lax.fori_loop(1, 64, total_wait, 0)
        mtot[it, 0] = jnp.sum(mbuf[it], axis=0)
        exchange = remote(
            mtot.at[it, 0], mtot.at[it, 1], mts_sem.at[it], mtr_sem.at[it], dev(s, y, 1 - k)
        )
        exchange.start()
        exchange.wait()
        grand = jnp.sum(mtot[it, 0] + mtot[it, 1])
        return jnp.full((8, 128), grand / CELLS, F32)

    def p_wait(src):
        src_dev = dev(src // 4, src % 4, k)

        @pl.when(src != me)
        def _():
            remote(
                prf.at[src], prf.at[src], qs_sem.at[src, 0], qr_sem.at[src, 0], src_dev
            ).wait_recv()
            remote(
                prp.at[src], prp.at[src], qs_sem.at[src, 1], qr_sem.at[src, 1], src_dev
            ).wait_recv()

    def update(scale, group, _):
        ys = group // 8
        even = ((group % 8) * 2) * 4 + ys
        odd = even + 4
        p_wait(even)
        p_wait(odd)
        a, b = prp[even].astype(F32), prp[odd].astype(F32)
        mid_top = jnp.where(mask48, a, swap(b))
        mid_bottom = jnp.where(mask48, swap(a), b)
        mid = jnp.concatenate(
            [mid_top.reshape(3, 16, 128), mid_bottom.reshape(3, 16, 128)], axis=1
        ).reshape(96, 128)
        first, third = prf[even].astype(F32), prf[odd].astype(F32)
        for t, value in enumerate((first.reshape(96, 128), mid, third.reshape(96, 128))):
            col = pl.multiple_of((group % 8) * 384 + t * 128, 128)
            before = prior_r[ys, :, :, pl.ds(col, 128)].reshape(96, 128)
            now = (MIX * value + (1.0 - MIX) * before) / scale
            xr[group * 3 + t, pl.ds(pl.multiple_of(k * 96, 16), 96), :] = now.astype(BF)

        @pl.when(group > 0)
        def _():
            forward_state(group - 1).start()

        return 0

    second_stage()
    stage5(0)
    for cp in gather_copies:
        cp.wait_send()
    m1 = first_stage(False, 0)
    scale = m1[0:1, :]
    lax.fori_loop(0, 32, functools.partial(update, scale), 0)
    forward_state(31).start()

    def p_sent(i, _):
        p_copies(i, False, end_send)
        return 0

    lax.fori_loop(0, 16, p_sent, 0)

    second_stage()
    mout[...] = first_stage(True, 1)

    def p_last(i, _):
        p_copies(i, True, end_send)
        return 0

    lax.fori_loop(0, 16, p_last, 0)

    def out_wait(i, _):
        src = (s + i) % 16
        remote(
            outf.at[src], outf.at[src], os_sem.at[src, 0], or_sem.at[src, 0], dev(src, y, k)
        ).wait_recv()
        remote(
            outp.at[src], outp.at[src], os_sem.at[src, 1], or_sem.at[src, 1], dev(src, y, k)
        ).wait_recv()
        return 0

    lax.fori_loop(1, 16, out_wait, 0)


def run_main(prior, t1, t2, c1, c2):
    any_spec = pl.BlockSpec(memory_space=pl.ANY)
    vmem = pl.BlockSpec(memory_space=pltpu.VMEM)
    dma = pltpu.SemaphoreType.DMA
    scratch = [
        pltpu.VMEM((4, 3, 32, 3072), F32),
        pltpu.VMEM((30720, 128), BF),
        pltpu.VMEM((4, 7680, 128), BF),
        pltpu.VMEM((96, 208, 128), BF),
        pltpu.VMEM((96, 128, 256), BF),
        pltpu.VMEM((48, 128, 128), BF),
        pltpu.VMEM((32, 2, 3, 32, 128), BF),
        pltpu.VMEM((32, 3, 32, 128), BF),
        pltpu.VMEM((48, 128, 128), BF),
        pltpu.VMEM((16, 4, 48, 128), BF),
        pltpu.VMEM((3, 128, 128), F32),
        pltpu.VMEM((64, 3, 32, 128), BF),
        pltpu.VMEM((64, 48, 128), BF),
        pltpu.VMEM((2, 64, 8, 128), F32),
        pltpu.VMEM((8, 128), F32),
        pltpu.VMEM((2, 2, 8, 128), F32),
        pltpu.VMEM((8, 128), F32),
        pltpu.VMEM((16, 8, 128), jnp.int32),
        pltpu.VMEM((4, 24, 128), jnp.int32),
        pltpu.SMEM((16, 8, 128), jnp.int32),
        pltpu.SMEM((4, 24, 128), jnp.int32),
        dma((7,)), dma((4,)), dma((4,)), dma((20,)), dma((20,)), dma((4,)), dma((4,)),
        dma((2, 2, 5, 4)), dma((2, 2, 5, 4)), dma((32,)), dma((32,)),
        dma((32, 2, 2)), dma((64, 2)), dma((64, 2)), dma((64, 2)),
        dma((64, 2)), dma((64, 2)), dma((16, 2)), dma((16, 2)),
        dma((64,)), dma((64,)), dma((2,)), dma((2,)),
    ]
    return pl.pallas_call(
        main_kernel,
        out_shape=(
            jax.ShapeDtypeStruct((16, 3, 128, 128), BF),
            jax.ShapeDtypeStruct((16, 4, 48, 128), BF),
            jax.ShapeDtypeStruct((8, 128), F32),
        ),
        in_specs=[any_spec, any_spec, any_spec, vmem, vmem],
        out_specs=(any_spec, any_spec, vmem),
        scratch_shapes=scratch,
        compiler_params=pltpu.CompilerParams(
            collective_id=0, has_side_effects=True, vmem_limit_bytes=60 << 20
        ),
        name="align",
    )(prior, t1, t2, c1, c2)


def combine_kernel(pf, pp, m, prior, out):
    mask = half_lanes((192, 128))
    scale = m[0:1, :]
    a, b = pp[0].astype(F32), pp[1].astype(F32)
    mid = jnp.concatenate([jnp.where(mask, a, swap(b)), jnp.where(mask, swap(a), b)], axis=0)
    for t, value in enumerate((pf[0].astype(F32), mid, pf[1].astype(F32))):
        cols = slice(t * 128, (t + 1) * 128)
        out[:, cols] = (MIX * value + (1.0 - MIX) * prior[:, cols]) / scale


def combine(pf, pp, m, prior):
    return pl.pallas_call(
        combine_kernel,
        grid=(8,),
        out_shape=jax.ShapeDtypeStruct((384, 3072), F32),
        in_specs=[
            pl.BlockSpec((2, 384, 128), lambda i: (i, 0, 0)),
            pl.BlockSpec((2, 192, 128), lambda i: (i, 0, 0)),
            pl.BlockSpec((8, 128), lambda i: (0, 0)),
            pl.BlockSpec((384, 384), lambda i: (0, i)),
        ],
        out_specs=pl.BlockSpec((384, 384), lambda i: (0, i)),
        name="combine",
    )(pf, pp, m, prior)


def local(prior_scores, tiles_first, columns_first, tiles_second, columns_second):
    t1 = tiles_first.reshape(1920, 128)
    t2 = tiles_second.reshape(15360, 128)
    c1 = jnp.pad(columns_first.astype(jnp.int32), ((0, 5), (0, 123)))
    c2 = jnp.pad(columns_second.astype(jnp.int32), ((0, 0), (0, 123)))
    pf, pp, m = run_main(prior_scores.reshape(3, 128, 3072), t1, t2, c1, c2)
    return combine(
        pf.reshape(16, 384, 128), pp.reshape(16, 192, 128), m, prior_scores
    )


def solution(mesh):
    return jax.shard_map(
        local,
        mesh=mesh,
        in_specs=(
            P("row", "col"),
            P("row", None, None, None),
            P("row", None),
            P("col", None, None, None),
            P("col", None),
        ),
        out_specs=P("row", "col"),
        check_vma=False,
    )
```

time: 642 us -> 290 us (0.45); the launches traced: 633 us -> 290 us
  Pallas kernels: 0 us -> 287 us
  blocking collectives: 213 us -> 0 us
  waiting for transfers between devices: 180 us -> 0 us
  local copies, waits for them, and re-layouts: 129 us -> 2.64 us
  matrix products: 44.8 us -> 0 us
  other arithmetic: 33.4 us -> 0 us
  starting transfers between devices: 16.9 us -> 0 us
  between operations: 15.6 us -> 0.01 us
    pallas_call x0 -> x2, Pallas kernels: none -> 287 us  [the longest x1 279 us: run_main(): pl.pallas_call(main_kernel, out_shape=(jax.ShapeDtypeStruct((16, 3, 128,...]
    all_gather x3 -> x0, waiting for transfers between devices: 179 us -> none  [the longest x2 179 us: local(): gathered = lax.all_gather(current, 'col', axis=0, tiled=True)]
    psum x8 -> x0, blocking collectives: 103 us -> none  [by_axis(): return functools.reduce(lax.psum, axes, value)]
    all_gather x1 -> x0, blocking collectives: 70.7 us -> none  [local(): lax.all_gather(columns_first, ROW, axis=0, tiled=True)]
    gather x4 -> x0, local copies, waits for them, and re-layouts: 54.8 us -> none  [the longest x2 29.8 us: first_product(): picked = jnp.take(blocks, columns, axis=1)]
    dot_general x4 -> x0, matrix products: 44.8 us -> none  [the longest x2 28.3 us: first_product(): jnp.einsum('cisk,isok->cio', picked, tile_set, preferred_element_type=jnp...]
    all_to_all x1 -> x0, blocking collectives: 39.2 us -> none  [local(): lax.all_to_all(mixed_cols, ROW, split_axis=0, concat_axis=1, tiled=True)]
    reshape x6 -> x0, local copies, waits for them, and re-layouts: 25.4 us -> none  [the longest x4 13.1 us: first_product(): blocks = slab_data.reshape(slab_data.shape[0], -1, tile_size)]
  transfers between devices with their start and end apart: 6 -> 0, of which waited for: 2 -> 0; matrix products, arithmetic and copies ran while one was open for 11% -> 0% of each run, Pallas kernels for 0% -> 0%
where the time goes in v1:
time: 290 us
  Pallas kernels  287 us (99%)
    pallas_call x1, Pallas kernels, run_main(): pl.pallas_call(main_kernel, out_shape=(jax.ShapeDtypeStruct((16, 3, 128,...  279 us
    pallas_call x1, Pallas kernels, combine(): pl.pallas_call(combine_kernel, grid=(8,), out_shape=jax.ShapeDtypeStruct(...  7.95 us

profile of v1, /device:TPU:1, one launch (start us, length us, event | category | flops | bytes accessed | tf_op | source)
XLA Modules:
  0.0 289.7 jit_solution(11639999086627209118)
XLA Ops:
  0.0 1.3 pad.8.c1
  1.3 0.8 copy.6
  2.0 0.6 pad.9.c2
  2.6 279.1 %align.1 = (bf16[16,3,128,128]{3,2,1,0:T(8,128)(2,1)}, bf16[16,4,48,128]{3,2,1,0:T(8,128)(2,1)}, f32[8,128]{1,0:T(8,128)}) custom-call(f32[3,128,3072]{2,1,0:T(8,128)} %bitcast.5, bf16[1920,128]{1,0:T(8,128)(2,1)} %bitcast.9, bf16[15360,128]{1,0:T(8,128)(2,1)} %bitcast.6, s32[8,128]{1,0:T(8,128)} %pad.8.c1, s32[24,128]{1,0:T(8,128)} %pad.9.c2), custom_call_target="tpu_custom_call" | custom-call | tf_op jit(solution)/shard_map/align/pallas_call | solution.py:651
  281.8 7.9 %combine.1 = f32[384,3072]{1,0:T(8,128)} custom-call(bf16[16,384,128]{2,1,0:T(8,128)(2,1)} %bitcast.7, bf16[16,192,128]{2,1,0:T(8,128)(2,1)} %bitcast.8, f32[8,128]{1,0:T(8,128)} %get-tuple-element.10.m, f32[384,3072]{1,0:T(8,128)} %prior.1), custom_call_target="tpu_custom_call" | custom-call | tf_op jit(solution)/shard_map/combine/pallas_call | solution.py:679

commit v2 on v1

--- a/solution.py
+++ b/solution.py
@@ -12,6 +12,7 @@
 F32 = jnp.float32
 MIX = 0.8
 CELLS = float(12288 * 12288)
+HELD = 8
 NT = (((1,), (1,)), ((), ()))
 NN = (((1,), (0,)), ((), ()))
 
@@ -28,7 +29,7 @@
     prior, t1, t2, c1, c2,
     outf, outp, mout,
     prior_r, a1, a2, xr, zc, zpk, zsend, zspk, pfull, ppk, ph, prf, prp,
-    mbuf, mpart, mtot, macc, c1g, c2g, c1s, c2s,
+    mbuf, msend, mpart, mtot, macc, c1g, c2g, c1s, c2s,
     lsem, ps_sem, pr_sem, cs_sem, cr_sem, ds_sem, dr_sem,
     gs_sem, gr_sem, xs_sem, xf_sem,
     zs_sem, zr_sem, fs_sem, ff_sem,
@@ -280,9 +281,11 @@
             ),
         )
 
+    ZG = x + 2 * z
+
     def z_copies(i, fn):
-        yd = (y + i // 4) % 4
-        g = (i + s) % 4
+        yd = (y + i) % 4
+        g = (i // 4 + ZG) % 4
         for d in range(2):
             sd = k * 8 + g * 2 + d
             slot = yd * 8 + g * 2 + d
@@ -317,9 +320,9 @@
         cp.wait_send()
 
     def z_compute(i, _):
-        yd = (y + i // 4) % 4
-        g = (i + s) % 4
-        yr = i // 4
+        yd = (y + i) % 4
+        g = (i // 4 + ZG) % 4
+        yr = i % 4
         values = []
         for t in range(3):
             jl = g * 3 + t
@@ -361,9 +364,15 @@
         )
         return full, packed
 
+    def z_source(n):
+        c = ((s % 8) // 2 + 4 - n // 16) % 4
+        r = (n // 4) % 4
+        xs = c % 2 + 2 * (r % 2)
+        zs = ((c + 4 - xs) // 2) % 2 + 2 * (r // 2)
+        return zs * 4 + xs, (y + 4 - n % 4) % 4
+
     def z_receive(i, _):
-        src_s = (s + i // 4) % 16
-        src_y = (y + i) % 4
+        src_s, src_y = z_source(i)
         src = src_s * 4 + src_y
         full, packed = z_forward(src_s, src_y)
         own = jnp.logical_and(src == me, s // 8 == k)
@@ -385,8 +394,7 @@
         return 0
 
     def z_finish(i, _):
-        src_s = (s + i // 4) % 16
-        src_y = (y + i) % 4
+        src_s, src_y = z_source(i)
         src = src_s * 4 + src_y
         full_at, packed_at = z_places(src_s, src_y, 1 - k)
         remote(
@@ -399,7 +407,8 @@
         ).wait()
         return 0
 
-    def z_unpack(i, _):
+    def z_unpack(n, _):
+        i = z_source((n // 3) * 4)[0] * 3 + n % 3
         packed = zpk[i].astype(F32)
         lane = lax.broadcasted_iota(jnp.int32, (128, 128), 1)
         fill = jnp.where(lane == 64, 1.0, 0.0).astype(F32)
@@ -412,18 +421,30 @@
         lax.fori_loop(0, 32, state_done, 0)
         lax.fori_loop(0, 16, z_compute, 0)
         z_copies(15, begin)
-        lax.fori_loop(0, 64, z_receive, 0)
-        lax.fori_loop(0, 64, z_finish, 0)
+        for phase in range(5):
+            if phase < 4:
+                lax.fori_loop(phase * 16, phase * 16 + 16, z_receive, 0)
+            if phase > 0:
+                lax.fori_loop(phase * 16 - 16, phase * 16, z_finish, 0)
+                lax.fori_loop(phase * 12 - 12, phase * 12, z_unpack, 0)
 
         def sent(i, _):
             z_copies(i, end_send)
             return 0
 
         lax.fori_loop(0, 16, sent, 0)
-        lax.fori_loop(0, 48, z_unpack, 0)
+
+    def partner_at(i, sign):
+        j = i // 2
+        dz = (j % 4) * (1 + 2 * k) * sign
+        xa = (x + 2 * ((j // 4 + j) % 2)) % 4
+        return ((z + dz) % 4) * 4 + xa + (i % 2) * (1 - 2 * (xa % 2))
+
+    def target(i):
+        return partner_at(i, 1)
 
     def p_copies(i, last, fn):
-        sd = (s + i) % 16
+        sd = target(i)
         if last:
             full = (pfull.at[pl.ds(sd * 3, 3)], outf.at[s])
             packed = (ppk.at[sd], outp.at[s])
@@ -450,11 +471,11 @@
                         cp.wait()
 
             return
-        for yd in range(4):
-            own = jnp.logical_and(sd == s, y == yd)
+        for step in range(4):
+            yd = (y + step) % 4
             pair = [
                 remote(
-                    pfull.at[pl.ds(sd * 3, 3), pl.ds(yd * 32, 32)], prf.at[me],
+                    pfull.at[pl.ds(sd * 3, 3), pl.ds(pl.multiple_of(yd * 32, 32), 32)], prf.at[me],
                     qs_sem.at[sd * 4 + yd, 0], qr_sem.at[me, 0], dev(sd, yd, k),
                 ),
                 remote(
@@ -463,20 +484,25 @@
                 ),
             ]
 
-            @pl.when(jnp.logical_not(own))
+            if step > 0:
+                for cp in pair:
+                    fn(cp)
+                continue
+
+            @pl.when(sd != s)
             def _():
                 for cp in pair:
                     fn(cp)
 
             if fn is begin:
 
-                @pl.when(own)
+                @pl.when(sd == s)
                 def _():
-                    prf[me] = pfull[pl.ds(sd * 3, 3), pl.ds(yd * 32, 32), :]
-                    prp[me] = ppk[sd, yd]
+                    prf[me] = pfull[pl.ds(sd * 3, 3), pl.ds(pl.multiple_of(y * 32, 32), 32), :]
+                    prp[me] = ppk[sd, y]
 
     def p_compute(last, i, _):
-        sd = (s + i) % 16
+        sd = target(i)
         for t in range(3):
             acc = None
             for slot in range(5):
@@ -504,7 +530,7 @@
                 high = ph[:, yd * 32 + 16 : yd * 32 + 32, :].reshape(48, 128)
             ppk[sd, yd] = (low + swap(high)).astype(BF)
 
-        @pl.when(i > 0)
+        @pl.when(jnp.logical_and(i > 0, i <= HELD))
         def _():
             p_copies(i - 1, last, begin)
 
@@ -513,14 +539,14 @@
     def first_stage(last, it):
         mpart[...] = jnp.zeros((8, 128), F32)
         lax.fori_loop(0, 16, functools.partial(p_compute, last), 0)
-        p_copies(15, last, begin)
-        mbuf[it, me] = MIX * mpart[...] + (1.0 - MIX) * macc[...]
-        mpart[...] = mbuf[it, me]
+        mine = jnp.sum(MIX * mpart[...] + (1.0 - MIX) * macc[...], axis=0, keepdims=True)
+        mbuf[it, me] = mine
+        msend[it] = mine
 
         def total_copy(i, src, dst):
             other = (me + i) % 64
             return remote(
-                mpart, mbuf.at[it, src], ms_sem.at[i], mr_sem.at[i], dev(dst // 4, dst % 4, k)
+                msend.at[it], mbuf.at[it, src], ms_sem.at[i], mr_sem.at[i], dev(dst // 4, dst % 4, k)
             )
 
         def total_send(i, _):
@@ -531,7 +557,12 @@
             total_copy(i, (me + 64 - i) % 64, (me + i) % 64).wait()
             return 0
 
+        def late(i, _):
+            p_copies(i, last, begin)
+            return 0
+
         lax.fori_loop(1, 64, total_send, 0)
+        lax.fori_loop(HELD, 16, late, 0)
         lax.fori_loop(1, 64, total_wait, 0)
         mtot[it, 0] = jnp.sum(mbuf[it], axis=0)
         exchange = remote(
@@ -540,7 +571,7 @@
         exchange.start()
         exchange.wait()
         grand = jnp.sum(mtot[it, 0] + mtot[it, 1])
-        return jnp.full((8, 128), grand / CELLS, F32)
+        return jnp.full((8, 128), CELLS / grand, F32)
 
     def p_wait(src):
         src_dev = dev(src // 4, src % 4, k)
@@ -554,7 +585,12 @@
                 prp.at[src], prp.at[src], qs_sem.at[src, 1], qr_sem.at[src, 1], src_dev
             ).wait_recv()
 
-    def update(scale, group, _):
+    def update_group(n):
+        src_s = partner_at((n // 4) * 2, 3)
+        return ((y + 4 - n % 4) % 4) * 8 + src_s // 2
+
+    def update(scale, n, _):
+        group = update_group(n)
         ys = group // 8
         even = ((group % 8) * 2) * 4 + ys
         odd = even + 4
@@ -570,12 +606,12 @@
         for t, value in enumerate((first.reshape(96, 128), mid, third.reshape(96, 128))):
             col = pl.multiple_of((group % 8) * 384 + t * 128, 128)
             before = prior_r[ys, :, :, pl.ds(col, 128)].reshape(96, 128)
-            now = (MIX * value + (1.0 - MIX) * before) / scale
+            now = (MIX * value + (1.0 - MIX) * before) * scale
             xr[group * 3 + t, pl.ds(pl.multiple_of(k * 96, 16), 96), :] = now.astype(BF)
 
-        @pl.when(group > 0)
+        @pl.when(n > 0)
         def _():
-            forward_state(group - 1).start()
+            forward_state(update_group(n - 1)).start()
 
         return 0
 
@@ -586,7 +622,7 @@
     m1 = first_stage(False, 0)
     scale = m1[0:1, :]
     lax.fori_loop(0, 32, functools.partial(update, scale), 0)
-    forward_state(31).start()
+    forward_state(update_group(31)).start()
 
     def p_sent(i, _):
         p_copies(i, False, end_send)
@@ -634,9 +670,10 @@
         pltpu.VMEM((3, 128, 128), F32),
         pltpu.VMEM((64, 3, 32, 128), BF),
         pltpu.VMEM((64, 48, 128), BF),
-        pltpu.VMEM((2, 64, 8, 128), F32),
+        pltpu.VMEM((2, 64, 1, 128), F32),
+        pltpu.VMEM((2, 1, 128), F32),
         pltpu.VMEM((8, 128), F32),
-        pltpu.VMEM((2, 2, 8, 128), F32),
+        pltpu.VMEM((2, 2, 1, 128), F32),
         pltpu.VMEM((8, 128), F32),
         pltpu.VMEM((16, 8, 128), jnp.int32),
         pltpu.VMEM((4, 24, 128), jnp.int32),
@@ -672,7 +709,7 @@
     mid = jnp.concatenate([jnp.where(mask, a, swap(b)), jnp.where(mask, swap(a), b)], axis=0)
     for t, value in enumerate((pf[0].astype(F32), mid, pf[1].astype(F32))):
         cols = slice(t * 128, (t + 1) * 128)
-        out[:, cols] = (MIX * value + (1.0 - MIX) * prior[:, cols]) / scale
+        out[:, cols] = (MIX * value + (1.0 - MIX) * prior[:, cols]) * scale
 
 
 def combine(pf, pp, m, prior):

time: 290 us -> 254 us (0.88)
  Pallas kernels: 287 us -> 251 us
    pallas_call x1, Pallas kernels: 279 us -> 243 us  [run_main(): pl.pallas_call(main_kernel, out_shape=(jax.ShapeDtypeStruct((16, 3, 128,...]
where the time goes in v2:
time: 254 us
  Pallas kernels  251 us (99%)
  local copies, waits for them, and re-layouts  2.64 us (1%)
    pallas_call x1, Pallas kernels, run_main(): pl.pallas_call(main_kernel, out_shape=(jax.ShapeDtypeStruct((16, 3, 128,...  243 us
    pallas_call x1, Pallas kernels, combine(): pl.pallas_call(combine_kernel, grid=(8,), out_shape=jax.ShapeDtypeStruct(...  7.95 us

profile of v2, /device:TPU:1, one launch (start us, length us, event | category | flops | bytes accessed | tf_op | source)
XLA Modules:
  0.0 253.8 jit_solution(17245252837260611964)
XLA Ops:
  0.0 1.3 pad.8.c1
  1.3 0.8 copy.6
  2.0 0.6 pad.9.c2
  2.6 243.2 %align.1 = (bf16[16,3,128,128]{3,2,1,0:T(8,128)(2,1)}, bf16[16,4,48,128]{3,2,1,0:T(8,128)(2,1)}, f32[8,128]{1,0:T(8,128)}) custom-call(f32[3,128,3072]{2,1,0:T(8,128)} %bitcast.5, bf16[1920,128]{1,0:T(8,128)(2,1)} %bitcast.9, bf16[15360,128]{1,0:T(8,128)(2,1)} %bitcast.6, s32[8,128]{1,0:T(8,128)} %pad.8.c1, s32[24,128]{1,0:T(8,128)} %pad.9.c2), custom_call_target="tpu_custom_call" | custom-call | tf_op jit(solution)/shard_map/align/pallas_call | solution.py:688
  245.9 7.9 %combine.1 = f32[384,3072]{1,0:T(8,128)} custom-call(bf16[16,384,128]{2,1,0:T(8,128)(2,1)} %bitcast.7, bf16[16,192,128]{2,1,0:T(8,128)(2,1)} %bitcast.8, f32[8,128]{1,0:T(8,128)} %get-tuple-element.10.m, f32[384,3072]{1,0:T(8,128)} %prior.1), custom_call_target="tpu_custom_call" | custom-call | tf_op jit(solution)/shard_map/combine/pallas_call | solution.py:716

commit v3 on v2

--- a/solution.py
+++ b/solution.py
@@ -29,11 +29,8 @@
     prior, t1, t2, c1, c2,
     outf, outp, mout,
     prior_r, a1, a2, xr, zc, zpk, zsend, zspk, pfull, ppk, ph, prf, prp,
-    mbuf, msend, mpart, mtot, macc, c1g, c2g, c1s, c2s,
-    lsem, ps_sem, pr_sem, cs_sem, cr_sem, ds_sem, dr_sem,
-    gs_sem, gr_sem, xs_sem, xf_sem,
-    zs_sem, zr_sem, fs_sem, ff_sem,
-    qs_sem, qr_sem, os_sem, or_sem, ms_sem, mr_sem, mts_sem, mtr_sem,
+    mbuf, msend, mpart, mtot, macc, c1p, c2p, c1g, c2g, c1s, c2s,
+    lsem, ss, sr, gr_sem, zr_sem, ff_sem, qr_sem,
 ):
     row = lax.axis_index("row")
     y = lax.axis_index("col")
@@ -51,6 +48,13 @@
             src_ref=src, dst_ref=dst, send_sem=ssem, recv_sem=rsem,
             device_id=target, device_id_type=MESH,
         )
+
+    def all_of(ref, number):
+        return remote(ref, ref, ss.at[number], sr.at[number], dev(s, y, 1 - k))
+
+    def rows_of(count, send, recv):
+        ref = a1.at[pl.ds(0, count)]
+        return remote(ref, ref, send, recv, dev(s, y, 1 - k))
 
     barrier = pltpu.get_barrier_semaphore()
 
@@ -70,24 +74,23 @@
     )
     load3.start()
     lax.fori_loop(1, 128, greet, 0)
-    c1g[s] = c1[...]
-    c2g[y] = c2[...]
+    c1p[0:3, 0:5] = c1[...]
+    c2p[:, 0:5] = c2[...]
+    c1g[s] = c1p[...]
+    c2g[y] = c2p[...]
     xr[:, 192:208, :] = jnp.ones((96, 16, 128), BF)
     pl.semaphore_wait(barrier, 127)
 
-    slice_copies, prior_copies, col_copies = [], [], []
     for d in (1, 3, 2):
         yd = (y + d) % 4
         cp = remote(
             t2.at[pl.ds(k * 7680 + s * 480, 480)],
             a2.at[(4 - d) % 4, pl.ds(s * 480, 480)],
-            ds_sem.at[d], dr_sem.at[d], dev(s, yd, k),
+            ss.at[2], sr.at[2], dev(s, yd, k),
         )
         cp.start()
-        slice_copies.append(cp)
-        cc = remote(c2, c2g.at[y], cs_sem.at[16 + d], cr_sem.at[16 + d], dev(s, yd, k))
+        cc = remote(c2p, c2g.at[y], ss.at[1], sr.at[1], dev(s, yd, k))
         cc.start()
-        col_copies.append(cc)
 
     XP, XM = (z * 4 + (x + 1) % 4), (z * 4 + (x + 3) % 4)
     ZP, ZM = (((z + 1) % 4) * 4 + x), (((z + 3) % 4) * 4 + x)
@@ -108,21 +111,18 @@
             return oz * 4 + (ox + delta) % 4
         return ((oz + delta) % 4) * 4 + ox
 
-    gather_copies = []
-
     def hop(kind, half, group, slot, origin, part, axis, up):
         cp = remote(
             region(kind, origin, part), region(kind, origin, part),
-            gs_sem.at[kind, half, group, slot], gr_sem.at[kind, half, group, slot],
+            ss.at[4 + kind], gr_sem.at[kind, half, group, slot],
             dev(nbr(axis, up), y, k),
         )
         cp.start()
-        gather_copies.append(cp)
 
     def landed(kind, half, group, slot, origin, part):
         cp = remote(
             region(kind, origin, part), region(kind, origin, part),
-            gs_sem.at[kind, half, group, slot], gr_sem.at[kind, half, group, slot],
+            ss.at[4 + kind], gr_sem.at[kind, half, group, slot],
             dev(nbr(0, True), y, k),
         )
         cp.wait_recv()
@@ -179,21 +179,19 @@
         yd = (y + d) % 4
         cp = remote(
             prior.at[:, pl.ds(pl.multiple_of(yd * 32, 32), 32), :], prior_r.at[y],
-            ps_sem.at[d], pr_sem.at[d], dev(s, yd, k),
+            ss.at[3], sr.at[3], dev(s, yd, k),
         )
         cp.start()
-        prior_copies.append(cp)
 
     def send_columns(i, _):
         remote(
-            c1, c1g.at[s], cs_sem.at[i], cr_sem.at[i], dev((s + i) % 16, y, k)
+            c1p, c1g.at[s], ss.at[0], sr.at[0], dev((s + i) % 16, y, k)
         ).start()
         return 0
 
     lax.fori_loop(1, 16, send_columns, 0)
 
-    for cp in slice_copies:
-        cp.wait()
+    all_of(a2.at[pl.ds(1, 3), pl.ds(0, 480)], 2).wait()
     stage1(1)
     stage2(0)
     stage2(1)
@@ -202,16 +200,8 @@
     load3.wait()
     load2.wait()
 
-    for cc in col_copies:
-        cc.wait()
-
-    def wait_columns(i, _):
-        remote(
-            c1, c1g.at[(s + 16 - i) % 16], cs_sem.at[i], cr_sem.at[i], dev((s + i) % 16, y, k)
-        ).wait()
-        return 0
-
-    lax.fori_loop(1, 16, wait_columns, 0)
+    all_of(c2g.at[pl.ds(0, 3)], 1).wait()
+    all_of(c1g.at[pl.ds(0, 15)], 0).wait()
     cps = [
         pltpu.make_async_copy(c1g, c1s, lsem.at[3]),
         pltpu.make_async_copy(c2g, c2s, lsem.at[4]),
@@ -223,8 +213,7 @@
 
     stage4(1)
     stage4(0)
-    for cp in prior_copies:
-        cp.wait()
+    all_of(prior_r.at[pl.ds(0, 3)], 3).wait()
 
     mask96 = half_lanes((96, 128))
     mask48 = half_lanes((48, 128))
@@ -233,15 +222,11 @@
         return remote(
             xr.at[pl.ds(group * 3, 3), pl.ds(k * 96, 96)],
             xr.at[pl.ds(group * 3, 3), pl.ds(k * 96, 96)],
-            xs_sem.at[group], xf_sem.at[group], dev(s, y, 1 - k),
-        )
-
-    def state_wait(group):
-        remote(
-            xr.at[pl.ds(group * 3, 3), pl.ds((1 - k) * 96, 96)],
-            xr.at[pl.ds(group * 3, 3), pl.ds((1 - k) * 96, 96)],
-            xs_sem.at[group], xf_sem.at[group], dev(s, y, 1 - k),
-        ).wait()
+            ss.at[6], sr.at[6], dev(s, y, 1 - k),
+        )
+
+    def state_wait():
+        all_of(xr.at[:, pl.ds(pl.multiple_of((1 - k) * 96, 16), 96)], 6).wait()
 
     macc[...] = jnp.zeros((8, 128), F32)
 
@@ -262,10 +247,6 @@
     lax.fori_loop(0, 32, convert, 0)
     forward_state(31).start()
     stage5(1)
-
-    def state_done(group, _):
-        state_wait(group)
-        return 0
 
     def z_places(src_s, src_y, p):
         return (
@@ -275,16 +256,17 @@
                 pl.ds(0, 128),
             ),
             (
+                p,
                 pl.ds(src_s * 3, 3),
-                pl.ds(pl.multiple_of(src_y * 32 + p * 16, 16), 16),
+                pl.ds(pl.multiple_of(src_y * 16, 16), 16),
                 pl.ds(0, 128),
             ),
         )
 
     ZG = x + 2 * z
 
-    def z_copies(i, fn):
-        yd = (y + i) % 4
+    def z_copies(i):
+        yd = (y + i * (1 + 2 * k)) % 4
         g = (i // 4 + ZG) % 4
         for d in range(2):
             sd = k * 8 + g * 2 + d
@@ -294,35 +276,27 @@
                 full_at, packed_at = z_places(s, y, p)
                 full = remote(
                     zsend.at[slot, p], zc.at[full_at],
-                    zs_sem.at[slot, p, 0], zr_sem.at[me, 0], dev(sd, yd, p),
+                    ss.at[7], zr_sem.at[s], dev(sd, yd, p),
                 )
                 packed = remote(
                     zspk.at[slot, :, pl.ds(p * 16, 16), :], zpk.at[packed_at],
-                    zs_sem.at[slot, p, 1], zr_sem.at[me, 1], dev(sd, yd, p),
+                    ss.at[7], zr_sem.at[s], dev(sd, yd, p),
                 )
 
                 @pl.when(jnp.logical_not(self_part))
                 def _():
-                    fn(full)
-                    fn(packed)
-
-                if fn is begin:
-
-                    @pl.when(self_part)
-                    def _():
-                        zc[full_at] = zsend[slot, p]
-                        zpk[packed_at] = zspk[slot, :, p * 16 : p * 16 + 16, :]
-
-    def begin(cp):
-        cp.start()
-
-    def end_send(cp):
-        cp.wait_send()
+                    full.start()
+                    packed.start()
+
+                @pl.when(self_part)
+                def _():
+                    zc[full_at] = zsend[slot, p]
+                    zpk[packed_at] = zspk[slot, :, p * 16 : p * 16 + 16, :]
 
     def z_compute(i, _):
-        yd = (y + i) % 4
+        yd = (y + i * (1 + 2 * k)) % 4
         g = (i // 4 + ZG) % 4
-        yr = i % 4
+        yr = (i * (1 + 2 * k)) % 4
         values = []
         for t in range(3):
             jl = g * 3 + t
@@ -347,69 +321,48 @@
 
         @pl.when(i > 0)
         def _():
-            z_copies(i - 1, begin)
-
-        return 0
-
-    def z_forward(src_s, src_y):
-        src = src_s * 4 + src_y
-        full_at, packed_at = z_places(src_s, src_y, k)
-        full = remote(
-            zc.at[full_at], zc.at[full_at],
-            fs_sem.at[src, 0], ff_sem.at[src, 0], dev(s, y, 1 - k),
-        )
-        packed = remote(
-            zpk.at[packed_at], zpk.at[packed_at],
-            fs_sem.at[src, 1], ff_sem.at[src, 1], dev(s, y, 1 - k),
-        )
-        return full, packed
+            z_copies(i - 1)
+
+        return 0
+
+    def z_forward(src_s, p):
+        full, packed = pl.ds((src_s * 2 + p) * 3, 3), pl.ds(src_s * 3, 3)
+        return [
+            remote(ref, ref, ss.at[8], ff_sem.at[src_s], dev(s, y, 1 - k))
+            for ref in (zc.at[full, :, pl.ds(0, 128)], zpk.at[p, packed])
+        ]
 
     def z_source(n):
         c = ((s % 8) // 2 + 4 - n // 16) % 4
         r = (n // 4) % 4
         xs = c % 2 + 2 * (r % 2)
         zs = ((c + 4 - xs) // 2) % 2 + 2 * (r // 2)
-        return zs * 4 + xs, (y + 4 - n % 4) % 4
+        return zs * 4 + xs
 
     def z_receive(i, _):
-        src_s, src_y = z_source(i)
-        src = src_s * 4 + src_y
-        full, packed = z_forward(src_s, src_y)
-        own = jnp.logical_and(src == me, s // 8 == k)
+        src_s = z_source(i * 4)
+        own = jnp.logical_and(src_s == s, s // 8 == k)
+
+        @pl.when(own)
+        def _():
+            rows_of(432, ss.at[7], zr_sem.at[src_s]).wait_recv()
 
         @pl.when(jnp.logical_not(own))
         def _():
-            full_at, packed_at = z_places(src_s, src_y, k)
-            remote(
-                zc.at[full_at], zc.at[full_at],
-                fs_sem.at[src, 0], zr_sem.at[src, 0], dev(s, y, 1 - k),
-            ).wait_recv()
-            remote(
-                zpk.at[packed_at], zpk.at[packed_at],
-                fs_sem.at[src, 1], zr_sem.at[src, 1], dev(s, y, 1 - k),
-            ).wait_recv()
-
-        full.start()
-        packed.start()
+            rows_of(576, ss.at[7], zr_sem.at[src_s]).wait_recv()
+
+        for cp in z_forward(src_s, k):
+            cp.start()
         return 0
 
     def z_finish(i, _):
-        src_s, src_y = z_source(i)
-        src = src_s * 4 + src_y
-        full_at, packed_at = z_places(src_s, src_y, 1 - k)
-        remote(
-            zc.at[full_at], zc.at[full_at],
-            fs_sem.at[src, 0], ff_sem.at[src, 0], dev(s, y, 1 - k),
-        ).wait()
-        remote(
-            zpk.at[packed_at], zpk.at[packed_at],
-            fs_sem.at[src, 1], ff_sem.at[src, 1], dev(s, y, 1 - k),
-        ).wait()
+        rows_of(576, ss.at[8], ff_sem.at[z_source(i * 4)]).wait_recv()
         return 0
 
     def z_unpack(n, _):
-        i = z_source((n // 3) * 4)[0] * 3 + n % 3
-        packed = zpk[i].astype(F32)
+        i = z_source((n // 3) * 4) * 3 + n % 3
+        parts = [zpk[p, i].astype(F32).reshape(4, 16, 128) for p in range(2)]
+        packed = jnp.concatenate(parts, axis=1).reshape(128, 128)
         lane = lax.broadcasted_iota(jnp.int32, (128, 128), 1)
         fill = jnp.where(lane == 64, 1.0, 0.0).astype(F32)
         block = (i // 3) * 6 + i % 3
@@ -418,21 +371,27 @@
         return 0
 
     def second_stage():
-        lax.fori_loop(0, 32, state_done, 0)
+        state_wait()
         lax.fori_loop(0, 16, z_compute, 0)
-        z_copies(15, begin)
+        z_copies(15)
         for phase in range(5):
             if phase < 4:
-                lax.fori_loop(phase * 16, phase * 16 + 16, z_receive, 0)
+                lax.fori_loop(phase * 4, phase * 4 + 4, z_receive, 0)
             if phase > 0:
-                lax.fori_loop(phase * 16 - 16, phase * 16, z_finish, 0)
+                lax.fori_loop(phase * 4 - 4, phase * 4, z_finish, 0)
                 lax.fori_loop(phase * 12 - 12, phase * 12, z_unpack, 0)
 
-        def sent(i, _):
-            z_copies(i, end_send)
-            return 0
-
-        lax.fori_loop(0, 16, sent, 0)
+        own = s // 8 == k
+
+        @pl.when(own)
+        def _():
+            rows_of(32 * 288 - 144, ss.at[7], sr.at[4]).wait_send()
+
+        @pl.when(jnp.logical_not(own))
+        def _():
+            rows_of(32 * 288, ss.at[7], sr.at[4]).wait_send()
+
+        rows_of(16 * 576, ss.at[8], sr.at[4]).wait_send()
 
     def partner_at(i, sign):
         j = i // 2
@@ -443,14 +402,14 @@
     def target(i):
         return partner_at(i, 1)
 
-    def p_copies(i, last, fn):
+    def p_copies(i, last):
         sd = target(i)
         if last:
             full = (pfull.at[pl.ds(sd * 3, 3)], outf.at[s])
             packed = (ppk.at[sd], outp.at[s])
             pair = [
-                remote(*full, os_sem.at[sd, 0], or_sem.at[s, 0], dev(sd, y, k)),
-                remote(*packed, os_sem.at[sd, 1], or_sem.at[s, 1], dev(sd, y, k)),
+                remote(*full, ss.at[9], sr.at[9], dev(sd, y, k)),
+                remote(*packed, ss.at[9], sr.at[9], dev(sd, y, k)),
             ]
             mine = [
                 pltpu.make_async_copy(*full, lsem.at[5]),
@@ -460,15 +419,12 @@
             @pl.when(sd != s)
             def _():
                 for cp in pair:
-                    fn(cp)
+                    cp.start()
 
             @pl.when(sd == s)
             def _():
                 for cp in mine:
-                    if fn is begin:
-                        cp.start()
-                    else:
-                        cp.wait()
+                    cp.start()
 
             return
         for step in range(4):
@@ -476,30 +432,28 @@
             pair = [
                 remote(
                     pfull.at[pl.ds(sd * 3, 3), pl.ds(pl.multiple_of(yd * 32, 32), 32)], prf.at[me],
-                    qs_sem.at[sd * 4 + yd, 0], qr_sem.at[me, 0], dev(sd, yd, k),
+                    ss.at[9], qr_sem.at[y * 8 + s // 2], dev(sd, yd, k),
                 ),
                 remote(
                     ppk.at[sd, yd], prp.at[me],
-                    qs_sem.at[sd * 4 + yd, 1], qr_sem.at[me, 1], dev(sd, yd, k),
+                    ss.at[9], qr_sem.at[y * 8 + s // 2], dev(sd, yd, k),
                 ),
             ]
 
             if step > 0:
                 for cp in pair:
-                    fn(cp)
+                    cp.start()
                 continue
 
             @pl.when(sd != s)
             def _():
                 for cp in pair:
-                    fn(cp)
-
-            if fn is begin:
-
-                @pl.when(sd == s)
-                def _():
-                    prf[me] = pfull[pl.ds(sd * 3, 3), pl.ds(pl.multiple_of(y * 32, 32), 32), :]
-                    prp[me] = ppk[sd, y]
+                    cp.start()
+
+            @pl.when(sd == s)
+            def _():
+                prf[me] = pfull[pl.ds(sd * 3, 3), pl.ds(pl.multiple_of(y * 32, 32), 32), :]
+                prp[me] = ppk[sd, y]
 
     def p_compute(last, i, _):
         sd = target(i)
@@ -532,7 +486,7 @@
 
         @pl.when(jnp.logical_and(i > 0, i <= HELD))
         def _():
-            p_copies(i - 1, last, begin)
+            p_copies(i - 1, last)
 
         return 0
 
@@ -544,46 +498,40 @@
         msend[it] = mine
 
         def total_copy(i, src, dst):
-            other = (me + i) % 64
             return remote(
-                msend.at[it], mbuf.at[it, src], ms_sem.at[i], mr_sem.at[i], dev(dst // 4, dst % 4, k)
+                msend.at[it], mbuf.at[it, src], ss.at[10], sr.at[10], dev(dst // 4, dst % 4, k)
             )
 
         def total_send(i, _):
             total_copy(i, me, (me + i) % 64).start()
             return 0
 
-        def total_wait(i, _):
-            total_copy(i, (me + 64 - i) % 64, (me + i) % 64).wait()
-            return 0
-
         def late(i, _):
-            p_copies(i, last, begin)
+            p_copies(i, last)
             return 0
 
         lax.fori_loop(1, 64, total_send, 0)
         lax.fori_loop(HELD, 16, late, 0)
-        lax.fori_loop(1, 64, total_wait, 0)
+        all_of(mbuf.at[it, pl.ds(0, 63)], 10).wait()
         mtot[it, 0] = jnp.sum(mbuf[it], axis=0)
         exchange = remote(
-            mtot.at[it, 0], mtot.at[it, 1], mts_sem.at[it], mtr_sem.at[it], dev(s, y, 1 - k)
+            mtot.at[it, 0], mtot.at[it, 1], ss.at[11], sr.at[11], dev(s, y, 1 - k)
         )
         exchange.start()
         exchange.wait()
         grand = jnp.sum(mtot[it, 0] + mtot[it, 1])
         return jnp.full((8, 128), CELLS / grand, F32)
 
-    def p_wait(src):
-        src_dev = dev(src // 4, src % 4, k)
-
-        @pl.when(src != me)
-        def _():
-            remote(
-                prf.at[src], prf.at[src], qs_sem.at[src, 0], qr_sem.at[src, 0], src_dev
-            ).wait_recv()
-            remote(
-                prp.at[src], prp.at[src], qs_sem.at[src, 1], qr_sem.at[src, 1], src_dev
-            ).wait_recv()
+    def p_wait(group):
+        own = group == y * 8 + s // 2
+
+        @pl.when(own)
+        def _():
+            rows_of(144, ss.at[9], qr_sem.at[group]).wait_recv()
+
+        @pl.when(jnp.logical_not(own))
+        def _():
+            rows_of(288, ss.at[9], qr_sem.at[group]).wait_recv()
 
     def update_group(n):
         src_s = partner_at((n // 4) * 2, 3)
@@ -594,8 +542,7 @@
         ys = group // 8
         even = ((group % 8) * 2) * 4 + ys
         odd = even + 4
-        p_wait(even)
-        p_wait(odd)
+        p_wait(group)
         a, b = prp[even].astype(F32), prp[odd].astype(F32)
         mid_top = jnp.where(mask48, a, swap(b))
         mid_bottom = jnp.where(mask48, swap(a), b)
@@ -617,39 +564,21 @@
 
     second_stage()
     stage5(0)
-    for cp in gather_copies:
-        cp.wait_send()
+    rows_of(15 * 1920, ss.at[4], sr.at[4]).wait_send()
+    rows_of(15 * 1440, ss.at[5], sr.at[4]).wait_send()
     m1 = first_stage(False, 0)
     scale = m1[0:1, :]
     lax.fori_loop(0, 32, functools.partial(update, scale), 0)
     forward_state(update_group(31)).start()
 
-    def p_sent(i, _):
-        p_copies(i, False, end_send)
-        return 0
-
-    lax.fori_loop(0, 16, p_sent, 0)
+    rows_of(63 * 144, ss.at[9], sr.at[4]).wait_send()
 
     second_stage()
     mout[...] = first_stage(True, 1)
 
-    def p_last(i, _):
-        p_copies(i, True, end_send)
-        return 0
-
-    lax.fori_loop(0, 16, p_last, 0)
-
-    def out_wait(i, _):
-        src = (s + i) % 16
-        remote(
-            outf.at[src], outf.at[src], os_sem.at[src, 0], or_sem.at[src, 0], dev(src, y, k)
-        ).wait_recv()
-        remote(
-            outp.at[src], outp.at[src], os_sem.at[src, 1], or_sem.at[src, 1], dev(src, y, k)
-        ).wait_recv()
-        return 0
-
-    lax.fori_loop(1, 16, out_wait, 0)
+    rows_of(15 * 576, ss.at[9], sr.at[9]).wait()
+    pltpu.make_async_copy(pfull.at[pl.ds(s * 3, 3)], outf.at[s], lsem.at[5]).wait()
+    pltpu.make_async_copy(ppk.at[s], outp.at[s], lsem.at[6]).wait()
 
 
 def run_main(prior, t1, t2, c1, c2):
@@ -662,7 +591,7 @@
         pltpu.VMEM((4, 7680, 128), BF),
         pltpu.VMEM((96, 208, 128), BF),
         pltpu.VMEM((96, 128, 256), BF),
-        pltpu.VMEM((48, 128, 128), BF),
+        pltpu.VMEM((2, 48, 64, 128), BF),
         pltpu.VMEM((32, 2, 3, 32, 128), BF),
         pltpu.VMEM((32, 3, 32, 128), BF),
         pltpu.VMEM((48, 128, 128), BF),
@@ -675,15 +604,13 @@
         pltpu.VMEM((8, 128), F32),
         pltpu.VMEM((2, 2, 1, 128), F32),
         pltpu.VMEM((8, 128), F32),
+        pltpu.VMEM((8, 128), jnp.int32),
+        pltpu.VMEM((24, 128), jnp.int32),
         pltpu.VMEM((16, 8, 128), jnp.int32),
         pltpu.VMEM((4, 24, 128), jnp.int32),
         pltpu.SMEM((16, 8, 128), jnp.int32),
         pltpu.SMEM((4, 24, 128), jnp.int32),
-        dma((7,)), dma((4,)), dma((4,)), dma((20,)), dma((20,)), dma((4,)), dma((4,)),
-        dma((2, 2, 5, 4)), dma((2, 2, 5, 4)), dma((32,)), dma((32,)),
-        dma((32, 2, 2)), dma((64, 2)), dma((64, 2)), dma((64, 2)),
-        dma((64, 2)), dma((64, 2)), dma((16, 2)), dma((16, 2)),
-        dma((64,)), dma((64,)), dma((2,)), dma((2,)),
+        dma((7,)), dma((12,)), dma((12,)), dma((2, 2, 5, 4)), dma((16,)), dma((16,)), dma((32,)),
     ]
     return pl.pallas_call(
         main_kernel,
@@ -731,9 +658,9 @@
 def local(prior_scores, tiles_first, columns_first, tiles_second, columns_second):
     t1 = tiles_first.reshape(1920, 128)
     t2 = tiles_second.reshape(15360, 128)
-    c1 = jnp.pad(columns_first.astype(jnp.int32), ((0, 5), (0, 123)))
-    c2 = jnp.pad(columns_second.astype(jnp.int32), ((0, 0), (0, 123)))
-    pf, pp, m = run_main(prior_scores.reshape(3, 128, 3072), t1, t2, c1, c2)
+    pf, pp, m = run_main(
+        prior_scores.reshape(3, 128, 3072), t1, t2, columns_first, columns_second
+    )
     return combine(
         pf.reshape(16, 384, 128), pp.reshape(16, 192, 128), m, prior_scores
     )

time: 254 us -> 235 us (0.925)
  Pallas kernels: 251 us -> 234 us
    pallas_call x1, Pallas kernels: 243 us -> 226 us  [run_main(): pl.pallas_call(main_kernel, out_shape=(jax.ShapeDtypeStruct((16, 3, 128,...]
where the time goes in v3:
time: 235 us
  Pallas kernels  234 us (100%)
    pallas_call x1, Pallas kernels, run_main(): pl.pallas_call(main_kernel, out_shape=(jax.ShapeDtypeStruct((16, 3, 128,...  226 us
    pallas_call x1, Pallas kernels, combine(): pl.pallas_call(combine_kernel, grid=(8,), out_shape=jax.ShapeDtypeStruct(...  7.95 us

profile of v3, /device:TPU:1, one launch (start us, length us, event | category | flops | bytes accessed | tf_op | source)
XLA Modules:
  0.0 235.0 jit_solution(7882880007908663809)
XLA Ops:
  0.0 1.4 copy.6.c2
  1.4 225.7 %align.1 = (bf16[16,3,128,128]{3,2,1,0:T(8,128)(2,1)}, bf16[16,4,48,128]{3,2,1,0:T(8,128)(2,1)}, f32[8,128]{1,0:T(8,128)}) custom-call(f32[3,128,3072]{2,1,0:T(8,128)} %bitcast.5, bf16[1920,128]{1,0:T(8,128)(2,1)} %bitcast.9, bf16[15360,128]{1,0:T(8,128)(2,1)} %bitcast.6, s32[3,5]{1,0:T(4,128)} %c1.1, s32[24,5]{1,0:T(8,128)} %copy.6.c2), custom_call_target="tpu_custom_call" | custom-call | tf_op jit(solution)/shard_map/align/pallas_call | solution.py:615
  227.1 7.9 %combine.1 = f32[384,3072]{1,0:T(8,128)} custom-call(bf16[16,384,128]{2,1,0:T(8,128)(2,1)} %bitcast.7, bf16[16,192,128]{2,1,0:T(8,128)(2,1)} %bitcast.8, f32[8,128]{1,0:T(8,128)} %get-tuple-element.10.m, f32[384,3072]{1,0:T(8,128)} %prior.1), custom_call_target="tpu_custom_call" | custom-call | tf_op jit(solution)/shard_map/combine/pallas_call | solution.py:643

commit v4 on v3

--- a/solution.py
+++ b/solution.py
@@ -13,6 +13,7 @@
 MIX = 0.8
 CELLS = float(12288 * 12288)
 HELD = 8
+CQ = 2
 NT = (((1,), (1,)), ((), ()))
 NN = (((1,), (0,)), ((), ()))
 
@@ -30,7 +31,7 @@
     outf, outp, mout,
     prior_r, a1, a2, xr, zc, zpk, zsend, zspk, pfull, ppk, ph, prf, prp,
     mbuf, msend, mpart, mtot, macc, c1p, c2p, c1g, c2g, c1s, c2s,
-    lsem, ss, sr, gr_sem, zr_sem, ff_sem, qr_sem,
+    rounds, lsem, ss, sr, gr_sem, zr_sem, ff_sem, qr_sem,
 ):
     row = lax.axis_index("row")
     y = lax.axis_index("col")
@@ -56,14 +57,17 @@
         ref = a1.at[pl.ds(0, count)]
         return remote(ref, ref, send, recv, dev(s, y, 1 - k))
 
+    x_line = [dev(z * 4 + (x + d) % 4, y, k) for d in (1, 2, 3)]
+    z_line = [dev(((z + d) % 4) * 4 + x, y, k) for d in (1, 2, 3)]
+    y_line = [dev(s, (y + d) % 4, k) for d in (1, 2, 3)]
+    pair_line = [dev(s, y, 1 - k)]
+
+    def greet(sem, peers):
+        for peer in peers:
+            pl.semaphore_signal(sem, inc=1, device_id=peer, device_id_type=MESH)
+
     barrier = pltpu.get_barrier_semaphore()
-
-    def greet(i, _):
-        other = (row * 4 + y + i) % 128
-        pl.semaphore_signal(
-            barrier, inc=1, device_id={"row": other // 4, "col": other % 4}, device_id_type=MESH
-        )
-        return 0
+    greet(barrier, x_line + z_line + y_line + pair_line)
 
     load1 = pltpu.make_async_copy(t1, a1.at[pl.ds(s * 1920, 1920)], lsem.at[0])
     load1.start()
@@ -73,13 +77,13 @@
         prior.at[:, pl.ds(pl.multiple_of(y * 32, 32), 32), :], prior_r.at[y], lsem.at[2]
     )
     load3.start()
-    lax.fori_loop(1, 128, greet, 0)
     c1p[0:3, 0:5] = c1[...]
     c2p[:, 0:5] = c2[...]
     c1g[s] = c1p[...]
     c2g[y] = c2p[...]
     xr[:, 192:208, :] = jnp.ones((96, 16, 128), BF)
-    pl.semaphore_wait(barrier, 127)
+    pl.semaphore_wait(barrier, 10)
+    greet(rounds.at[0], x_line)
 
     for d in (1, 3, 2):
         yd = (y + d) % 4
@@ -189,16 +193,21 @@
         ).start()
         return 0
 
+    pl.semaphore_wait(rounds.at[0], 3)
+    greet(rounds.at[1], z_line)
     lax.fori_loop(1, 16, send_columns, 0)
 
     all_of(a2.at[pl.ds(1, 3), pl.ds(0, 480)], 2).wait()
     stage1(1)
+    stage2(1)
     stage2(0)
-    stage2(1)
+    stage3(1)
     stage3(0)
-    stage3(1)
     load3.wait()
     load2.wait()
+
+    pl.semaphore_wait(rounds.at[1], 3)
+    greet(rounds.at[2], pair_line)
 
     all_of(c2g.at[pl.ds(0, 3)], 1).wait()
     all_of(c1g.at[pl.ds(0, 15)], 0).wait()
@@ -212,6 +221,7 @@
         cp.wait()
 
     stage4(1)
+    pl.semaphore_wait(rounds.at[2], 1)
     stage4(0)
     all_of(prior_r.at[pl.ds(0, 3)], 3).wait()
 
@@ -610,6 +620,7 @@
         pltpu.VMEM((4, 24, 128), jnp.int32),
         pltpu.SMEM((16, 8, 128), jnp.int32),
         pltpu.SMEM((4, 24, 128), jnp.int32),
+        pltpu.SemaphoreType.REGULAR((3,)),
         dma((7,)), dma((12,)), dma((12,)), dma((2, 2, 5, 4)), dma((16,)), dma((16,)), dma((32,)),
     ]
     return pl.pallas_call(
@@ -632,6 +643,13 @@
 def combine_kernel(pf, pp, m, prior, out):
     mask = half_lanes((192, 128))
     scale = m[0:1, :]
+    for q in range(CQ):
+        cols = pl.ds(q * 384, 384)
+        pair = pl.ds(q * 2, 2)
+        combine_pair(pf.at[pair], pp.at[pair], scale, mask, prior.at[:, cols], out.at[:, cols])
+
+
+def combine_pair(pf, pp, scale, mask, prior, out):
     a, b = pp[0].astype(F32), pp[1].astype(F32)
     mid = jnp.concatenate([jnp.where(mask, a, swap(b)), jnp.where(mask, swap(a), b)], axis=0)
     for t, value in enumerate((pf[0].astype(F32), mid, pf[1].astype(F32))):
@@ -642,15 +660,15 @@
 def combine(pf, pp, m, prior):
     return pl.pallas_call(
         combine_kernel,
-        grid=(8,),
+        grid=(8 // CQ,),
         out_shape=jax.ShapeDtypeStruct((384, 3072), F32),
         in_specs=[
-            pl.BlockSpec((2, 384, 128), lambda i: (i, 0, 0)),
-            pl.BlockSpec((2, 192, 128), lambda i: (i, 0, 0)),
+            pl.BlockSpec((2 * CQ, 384, 128), lambda i: (i, 0, 0)),
+            pl.BlockSpec((2 * CQ, 192, 128), lambda i: (i, 0, 0)),
             pl.BlockSpec((8, 128), lambda i: (0, 0)),
-            pl.BlockSpec((384, 384), lambda i: (0, i)),
+            pl.BlockSpec((384, 384 * CQ), lambda i: (0, i)),
         ],
-        out_specs=pl.BlockSpec((384, 384), lambda i: (0, i)),
+        out_specs=pl.BlockSpec((384, 384 * CQ), lambda i: (0, i)),
         name="combine",
     )(pf, pp, m, prior)
 

time: 235 us -> 228 us (0.970)
  Pallas kernels: 234 us -> 226 us
    pallas_call x1, Pallas kernels: 226 us -> 220 us  [run_main(): pl.pallas_call(main_kernel, out_shape=(jax.ShapeDtypeStruct((16, 3, 128,...]
where the time goes in v4:
time: 228 us; the launch traced here: 227 us
  Pallas kernels  226 us (99%)
    pallas_call x1, Pallas kernels, run_main(): pl.pallas_call(main_kernel, out_shape=(jax.ShapeDtypeStruct((16, 3, 128,...  220 us
    pallas_call x1, Pallas kernels, combine(): pl.pallas_call(combine_kernel, grid=(8 // CQ,), out_shape=jax.ShapeDtypeS...  6.08 us

profile of v4, /device:TPU:1, one launch (start us, length us, event | category | flops | bytes accessed | tf_op | source)
XLA Modules:
  0.0 227.5 jit_solution(5908896554860032807)
XLA Ops:
  0.0 1.4 copy.6.c2
  1.4 220.0 %align.1 = (bf16[16,3,128,128]{3,2,1,0:T(8,128)(2,1)}, bf16[16,4,48,128]{3,2,1,0:T(8,128)(2,1)}, f32[8,128]{1,0:T(8,128)}) custom-call(f32[3,128,3072]{2,1,0:T(8,128)} %bitcast.5, bf16[1920,128]{1,0:T(8,128)(2,1)} %bitcast.9, bf16[15360,128]{1,0:T(8,128)(2,1)} %bitcast.6, s32[3,5]{1,0:T(4,128)} %c1.1, s32[24,5]{1,0:T(8,128)} %copy.6.c2), custom_call_target="tpu_custom_call" | custom-call | tf_op jit(solution)/shard_map/align/pallas_call | solution.py:626
  221.4 6.1 %combine.1 = f32[384,3072]{1,0:T(8,128)} custom-call(bf16[16,384,128]{2,1,0:T(8,128)(2,1)} %bitcast.7, bf16[16,192,128]{2,1,0:T(8,128)(2,1)} %bitcast.8, f32[8,128]{1,0:T(8,128)} %get-tuple-element.10.m, f32[384,3072]{1,0:T(8,128)} %prior.1), custom_call_target="tpu_custom_call" | custom-call | tf_op jit(solution)/shard_map/combine/pallas_call | solution.py:661

commit v5 on v4

--- a/solution.py
+++ b/solution.py
@@ -13,7 +13,7 @@
 MIX = 0.8
 CELLS = float(12288 * 12288)
 HELD = 8
-CQ = 2
+CQ = 4
 NT = (((1,), (1,)), ((), ()))
 NN = (((1,), (0,)), ((), ()))
 
@@ -380,6 +380,12 @@
         zc[block + 3, :, 128:256] = jnp.where(lane < 64, swap(packed), fill).astype(BF)
         return 0
 
+    def z_complete(i, _):
+        z_finish(i, 0)
+        for t in range(3):
+            z_unpack(i * 3 + t, 0)
+        return 0
+
     def second_stage():
         state_wait()
         lax.fori_loop(0, 16, z_compute, 0)
@@ -388,8 +394,7 @@
             if phase < 4:
                 lax.fori_loop(phase * 4, phase * 4 + 4, z_receive, 0)
             if phase > 0:
-                lax.fori_loop(phase * 4 - 4, phase * 4, z_finish, 0)
-                lax.fori_loop(phase * 12 - 12, phase * 12, z_unpack, 0)
+                lax.fori_loop(phase * 4 - 4, phase * 4, z_complete, 0)
 
         own = s // 8 == k
 
@@ -405,7 +410,7 @@
 
     def partner_at(i, sign):
         j = i // 2
-        dz = (j % 4) * (1 + 2 * k) * sign
+        dz = ((j + 1) % 4) * (1 + 2 * k) * sign
         xa = (x + 2 * ((j // 4 + j) % 2)) % 4
         return ((z + dz) % 4) * 4 + xa + (i % 2) * (1 - 2 * (xa % 2))
 

time: 228 us -> 223 us (0.978)
  Pallas kernels: 226 us -> 221 us
    pallas_call x1, Pallas kernels: 220 us -> 216 us  [run_main(): pl.pallas_call(main_kernel, out_shape=(jax.ShapeDtypeStruct((16, 3, 128,...]
where the time goes in v5:
time: 223 us
  Pallas kernels  221 us (99%)
    pallas_call x1, Pallas kernels, run_main(): pl.pallas_call(main_kernel, out_shape=(jax.ShapeDtypeStruct((16, 3, 128,...  216 us
    pallas_call x1, Pallas kernels, combine(): pl.pallas_call(combine_kernel, grid=(8 // CQ,), out_shape=jax.ShapeDtypeS...  5.28 us

profile of v5, /device:TPU:1, one launch (start us, length us, event | category | flops | bytes accessed | tf_op | source)
XLA Modules:
  0.0 222.6 jit_solution(7062492811441800677)
XLA Ops:
  0.0 1.4 copy.6.c2
  1.4 216.0 %align.1 = (bf16[16,3,128,128]{3,2,1,0:T(8,128)(2,1)}, bf16[16,4,48,128]{3,2,1,0:T(8,128)(2,1)}, f32[8,128]{1,0:T(8,128)}) custom-call(f32[3,128,3072]{2,1,0:T(8,128)} %bitcast.5, bf16[1920,128]{1,0:T(8,128)(2,1)} %bitcast.9, bf16[15360,128]{1,0:T(8,128)(2,1)} %bitcast.6, s32[3,5]{1,0:T(4,128)} %c1.1, s32[24,5]{1,0:T(8,128)} %copy.6.c2), custom_call_target="tpu_custom_call" | custom-call | tf_op jit(solution)/shard_map/align/pallas_call | solution.py:631
  217.3 5.3 %combine.1 = f32[384,3072]{1,0:T(8,128)} custom-call(bf16[16,384,128]{2,1,0:T(8,128)(2,1)} %bitcast.7, bf16[16,192,128]{2,1,0:T(8,128)(2,1)} %bitcast.8, f32[8,128]{1,0:T(8,128)} %get-tuple-element.10.m, f32[384,3072]{1,0:T(8,128)} %prior.1), custom_call_target="tpu_custom_call" | custom-call | tf_op jit(solution)/shard_map/combine/pallas_call | solution.py:666

commit v6 on v5

--- a/solution.py
+++ b/solution.py
@@ -410,7 +410,7 @@
 
     def partner_at(i, sign):
         j = i // 2
-        dz = ((j + 1) % 4) * (1 + 2 * k) * sign
+        dz = ((j + 2) % 4) * (1 + 2 * k) * sign
         xa = (x + 2 * ((j // 4 + j) % 2)) % 4
         return ((z + dz) % 4) * 4 + xa + (i % 2) * (1 - 2 * (xa % 2))
 

time: 223 us -> 224 us (level)
  no operation moved by 1% of the time
where the time goes in v6:
time: 224 us; the launch traced here: 223 us
  Pallas kernels  222 us (99%)
    pallas_call x1, Pallas kernels, run_main(): pl.pallas_call(main_kernel, out_shape=(jax.ShapeDtypeStruct((16, 3, 128,...  217 us
    pallas_call x1, Pallas kernels, combine(): pl.pallas_call(combine_kernel, grid=(8 // CQ,), out_shape=jax.ShapeDtypeS...  5.28 us

profile of v6, /device:TPU:1, one launch (start us, length us, event | category | flops | bytes accessed | tf_op | source)
XLA Modules:
  0.0 223.4 jit_solution(11556464238357091726)
XLA Ops:
  0.0 1.4 copy.6.c2
  1.4 216.8 %align.1 = (bf16[16,3,128,128]{3,2,1,0:T(8,128)(2,1)}, bf16[16,4,48,128]{3,2,1,0:T(8,128)(2,1)}, f32[8,128]{1,0:T(8,128)}) custom-call(f32[3,128,3072]{2,1,0:T(8,128)} %bitcast.5, bf16[1920,128]{1,0:T(8,128)(2,1)} %bitcast.9, bf16[15360,128]{1,0:T(8,128)(2,1)} %bitcast.6, s32[3,5]{1,0:T(4,128)} %c1.1, s32[24,5]{1,0:T(8,128)} %copy.6.c2), custom_call_target="tpu_custom_call" | custom-call | tf_op jit(solution)/shard_map/align/pallas_call | solution.py:631
  218.2 5.3 %combine.1 = f32[384,3072]{1,0:T(8,128)} custom-call(bf16[16,384,128]{2,1,0:T(8,128)(2,1)} %bitcast.7, bf16[16,192,128]{2,1,0:T(8,128)(2,1)} %bitcast.8, f32[8,128]{1,0:T(8,128)} %get-tuple-element.10.m, f32[384,3072]{1,0:T(8,128)} %prior.1), custom_call_target="tpu_custom_call" | custom-call | tf_op jit(solution)/shard_map/combine/pallas_call | solution.py:666
